TPU v7x, 32 devices: a whole 2x2x4 slice. The times are simulated.
32 devices in a mesh: frame: 8 (over z, core), mp: 2 (over x), dp: 2 (over y).
Axes of the slice: x: 2, y: 2, z: 4, core: 2. Of those that a mesh axis runs over, the one named last changes fastest.
Arguments:
- tokens: bfloat16 [4, 8, 160, 5120], P('dp', 'frame', None, 'mp'), may hold values from -30 to 30
- token_mask: int32 [4, 8, 160], P('dp', 'frame'), may hold values 0 or 1
- mask_embed: bfloat16 [5120], P('mp'), may hold values from -6 to 6
- w_qkv: bfloat16 [5120, 3, 3072], P('frame', None, 'mp'), may hold values from -0.078125 to 0.078125
- w_out: bfloat16 [3072, 5120], P('mp'), may hold values from -0.109375 to 0.109375
- action_idx: int32 [4, 8], P('dp', 'frame'), may hold values from 0 to 7
- codebook: float32 [8, 32], replicated, may hold values from -6 to 6
- act_proj: float32 [32, 5120], P(None, 'mp'), may hold values from -1 to 1
- cotangent: bfloat16 [4, 8, 160, 5120], P('dp', 'frame', None, 'mp'), may hold values from -6 to 6
Outputs:
- next_state: bfloat16 [4, 8, 160, 5120], P('dp', 'frame', None, 'mp')
- grad_proj: float32 [32, 5120], P(None, 'mp')
All inputs are finite; a program needn't handle non-finite values. No bound on the sum of `token_mask` on one device may be relied on, other than what follows from the above.
Results may differ from a plain program's by a relative error of at most 0.0098.
Values may be sent and summed in bfloat16 or wider, within the bound.
A program may use at most 128 MiB of HBM per device.

v0:
```python
import functools
import math

import jax
import jax.numpy as jnp
from jax import lax
from jax.experimental import pallas as pl
from jax.experimental.pallas import tpu as pltpu
from jax.sharding import PartitionSpec as P

HS = 128


def attend_kernel(frames, q_ref, k_ref, v_ref, o_ref):
    scale = 1.0 / math.sqrt(HS)
    for t in range(frames):
        q = q_ref[t].astype(jnp.float32) * scale
        scores = [
            jnp.sum(q * k_ref[u].astype(jnp.float32), axis=-1, keepdims=True) for u in range(t + 1)
        ]
        peak = functools.reduce(jnp.maximum, scores)
        weights = [jnp.exp(s - peak) for s in scores]
        total = functools.reduce(jnp.add, weights)
        accum = functools.reduce(
            jnp.add, [w * v_ref[u].astype(jnp.float32) for u, w in enumerate(weights)]
        )
        o_ref[t] = (accum / total).astype(o_ref.dtype)


def attend(qkv, frames, heads_width):
    rows = qkv.shape[1]
    heads = heads_width // HS
    spec = lambda part: pl.BlockSpec((frames, rows, HS), lambda h, part=part: (0, 0, part * heads + h))
    return pl.pallas_call(
        functools.partial(attend_kernel, frames),
        grid=(heads,),
        in_specs=[spec(0), spec(1), spec(2)],
        out_specs=spec(0),
        out_shape=jax.ShapeDtypeStruct((frames, rows, heads_width), jnp.bfloat16),
        cost_estimate=pl.CostEstimate(flops=4 * frames * frames * rows * heads_width,
                                      bytes_accessed=8 * frames * rows * heads_width,
                                      transcendentals=0),
        name="attend",
    )(qkv, qkv, qkv)


def spread_kernel(frames, dps, x_ref, o_ref, send_sem, recv_sem, own_sem):
    count = frames * dps
    me = lax.axis_index("frame") * dps + lax.axis_index("dp")
    barrier = pltpu.get_barrier_semaphore()

    def peer(shift):
        other = lax.rem(me + shift, count)
        return {"frame": other // dps, "dp": lax.rem(other, dps)}

    for shift in range(1, count):
        pl.semaphore_signal(barrier, inc=1, device_id=peer(shift),
                            device_id_type=pl.DeviceIdType.MESH)
    own = pltpu.make_async_copy(x_ref, o_ref.at[me], own_sem)
    own.start()
    pl.semaphore_wait(barrier, count - 1)
    copies = []
    for shift in range(1, count):
        copy = pltpu.make_async_remote_copy(
            src_ref=x_ref, dst_ref=o_ref.at[me], send_sem=send_sem.at[shift],
            recv_sem=recv_sem.at[shift], device_id=peer(shift),
            device_id_type=pl.DeviceIdType.MESH)
        copy.start()
        copies.append(copy)
    own.wait()
    for copy in copies:
        copy.wait()


def spread_terms(terms, frames, dps):
    count = frames * dps
    return pl.pallas_call(
        functools.partial(spread_kernel, frames, dps),
        in_specs=[pl.BlockSpec(memory_space=pltpu.VMEM)],
        out_specs=pl.BlockSpec(memory_space=pltpu.VMEM),
        out_shape=jax.ShapeDtypeStruct((count, *terms.shape), terms.dtype),
        scratch_shapes=[pltpu.SemaphoreType.DMA((count,)), pltpu.SemaphoreType.DMA((count,)),
                        pltpu.SemaphoreType.DMA],
        compiler_params=pltpu.CompilerParams(collective_id=1, has_side_effects=True),
        name="spread_terms",
    )(terms)


def gather_mp(block, size):
    if size != 2:
        return lax.all_gather(block, "mp", axis=block.ndim - 1, tiled=True)
    other = lax.ppermute(block, "mp", [(0, 1), (1, 0)])
    first = lax.axis_index("mp") == 0
    return jnp.concatenate(
        [jnp.where(first, block, other), jnp.where(first, other, block)], axis=-1
    )


def body(mp_size, dp_size, tokens, token_mask, mask_embed, w_qkv, w_out, action_idx, codebook,
         act_proj, cotangent):
    clips, _, spots, width = tokens.shape
    heads_width = w_qkv.shape[2]
    depth = w_qkv.shape[0]
    xin = jnp.where(token_mask[..., None] == 1, mask_embed, tokens)
    share = depth // dp_size
    mine = lax.dynamic_slice_in_dim(
        w_qkv.reshape(depth, 3 * heads_width), lax.axis_index("dp") * share, share, axis=0
    )
    weights = lax.all_gather(mine, ("frame", "dp"), axis=0, tiled=True)
    if mp_size == 2:
        my_mp = lax.axis_index("mp")
        out_mine = lax.dynamic_slice_in_dim(w_out, my_mp * width, width, axis=1)
        out_other = lax.ppermute(
            lax.dynamic_slice_in_dim(w_out, (1 - my_mp) * width, width, axis=1),
            "mp", [(0, 1), (1, 0)])
    spread = lax.all_to_all(
        xin.reshape(clips, spots, width), "frame", split_axis=1, concat_axis=0, tiled=True
    )
    frames = spread.shape[0] // clips
    local = spread.shape[1]
    features = gather_mp(spread.reshape(frames * clips * local, width), mp_size)
    qkv = jnp.dot(features, weights, preferred_element_type=jnp.float32).astype(jnp.bfloat16)
    attn = attend(qkv.reshape(frames, clips * local, 3 * heads_width), frames, heads_width)
    back = lax.all_to_all(
        attn.reshape(frames * clips, local, heads_width), "frame", split_axis=0, concat_axis=1,
        tiled=True,
    )
    heads = back.reshape(clips * spots, heads_width)
    if mp_size == 2:
        other_heads = lax.ppermute(heads, "mp", [(0, 1), (1, 0)])
        mixed_rows = jnp.dot(heads, out_mine, preferred_element_type=jnp.float32) + jnp.dot(
            other_heads, out_other, preferred_element_type=jnp.float32)
    else:
        out_block = lax.all_to_all(w_out, "mp", split_axis=1, concat_axis=0, tiled=True)
        mixed_rows = jnp.dot(gather_mp(heads, mp_size), out_block,
                             preferred_element_type=jnp.float32)
    mixed = mixed_rows.reshape(clips, 1, spots, width)
    onehot = (
        action_idx.reshape(clips)[:, None] == jnp.arange(codebook.shape[0])[None, :]
    ).astype(jnp.float32)
    codevec = jnp.dot(onehot, codebook, precision=lax.Precision.HIGHEST)
    gate = jnp.dot(codevec, act_proj, precision=lax.Precision.HIGHEST)
    next_state = (xin.astype(jnp.float32) + gate[:, None, None, :] * mixed).astype(jnp.bfloat16)
    dgate = jnp.sum(cotangent.astype(jnp.float32) * mixed, axis=2).reshape(clips, width)
    codes = codevec.shape[1]
    padded = jnp.pad(codevec, ((0, 0), (0, -codes % 128)))
    terms = spread_terms(jnp.concatenate([dgate, padded], axis=1), frames, dp_size)
    terms = terms.reshape(frames * dp_size * clips, -1)
    grad_proj = jnp.dot(
        terms[:, width : width + codes].T, terms[:, :width], precision=lax.Precision.HIGHEST)
    return (next_state, grad_proj)


def solution(mesh):
    in_specs = (
        P("dp", "frame", None, "mp"),
        P("dp", "frame", None),
        P("mp"),
        P("frame", None, "mp"),
        P("mp", None),
        P("dp", "frame"),
        P(),
        P(None, "mp"),
        P("dp", "frame", None, "mp"),
    )
    out_specs = (P("dp", "frame", None, "mp"), P(None, "mp"))
    return jax.shard_map(
        functools.partial(body, mesh.shape["mp"], mesh.shape["dp"]),
        mesh=mesh, in_specs=in_specs, out_specs=out_specs, check_vma=False,
    )
```

profile of v0, /device:TPU:1, one launch (start us, length us, event | category | flops | bytes accessed | tf_op | source)
XLA Modules:
  0.0 441.1 jit_solution(3602925788211797718)
XLA Ops:
  7.2 0.0 copy-start
  7.2 0.0 all-gather.2.cloned.1.call-start
  7.2 9.0 %copy.22 = bf16[640,3,1536]{0,2,1:T(8,128)(2,1)} copy(bf16[640,3,1536]{2,0,1:T(8,128)(2,1)} %param.12) | data formatting | bytes 11796480 | tf_op args[3]
  16.2 6.2 %constant_dynamic-slice_fusion.1 = bf16[320,4608]{0,1:T(8,128)(2,1)} fusion(bf16[640,4608]{0,1:T(8,128)(2,1)} %bitcast.26, s32[]{:T(128)S(6)} %select_n.29), kind=kLoop, calls=%fused_computation.27 | loop fusion | bytes 5898244 | tf_op jit(solution)/shard_map/dynamic_slice | solution.py:106
  22.4 0.0 copy-start.7
  22.4 0.0 copy-start.2
  22.4 0.0 copy-start.6
  22.4 5.7 %copy.23 = bf16[320,4608]{1,0:T(8,128)(2,1)} copy(bf16[320,4608]{0,1:T(8,128)(2,1)} %constant_dynamic-slice_fusion.1) | data formatting | bytes 5898240 | tf_op jit(solution)/shard_map/dynamic_slice | solution.py:106
  28.1 0.0 all-gather.2.cloned.1.call-update
  28.1 0.0 copy-done.7
  28.1 0.1 copy.28
  28.3 0.0 copy-done.2
  28.3 0.0 copy-done.6
  28.3 3.2 fusion.9
  31.5 6.4 %all-to-all-start = ((bf16[2,160,2560]{2,0,1:T(2,128)(2,1)}), bf16[2,160,2560]{2,0,1:T(2,128)(2,1)S(1)}, u32[]{:S(2)}, u32[]{:S(2)}) async-start(bf16[2,160,2560]{2,0,1:T(2,128)(2,1)} %fusion.9), calls=%async_computation | async-start | bytes 3276800 | tf_op jit(solution)/shard_map/all_to_all | solution.py:116
  37.9 47.4 %all-to-all-done = bf16[2,160,2560]{2,0,1:T(2,128)(2,1)S(1)} async-done(((bf16[2,160,2560]{2,0,1:T(2,128)(2,1)}), bf16[2,160,2560]{2,0,1:T(2,128)(2,1)S(1)}, u32[]{:S(2)}, u32[]{:S(2)}) %all-to-all-start) | async-done | bytes 1638432 | tf_op jit(solution)/shard_map/all_to_all | solution.py:116
  85.3 0.0 copy-start.1
  85.3 1.2 copy-done.1
  86.4 1.7 copy.21
  88.1 1.3 reshape.60
  89.5 0.0 copy-start.4
  89.5 1.2 collective-permute-start
  90.7 7.1 %constant_dynamic-slice_fusion = bf16[1536,2560]{1,0:T(8,128)(2,1)} fusion(bf16[1536,5120]{1,0:T(8,128)(2,1)} %param.13, s32[]{:T(128)S(6)} %select_n.31), kind=kLoop, calls=%fused_computation.25 | loop fusion | bytes 15728644 | tf_op jit(solution)/shard_map/dynamic_slice | solution.py:114
  97.8 0.4 collective-permute-start.2
  98.1 28.1 %collective-permute-done = bf16[320,2560]{1,0:T(8,128)(2,1)} collective-permute-done((bf16[320,2560]{1,0:T(8,128)(2,1)}, bf16[320,2560]{1,0:T(8,128)(2,1)}, u32[]{:S(2)}, u32[]{:S(2)}) %collective-permute-start) | collective-permute-done | bytes 1638432 | tf_op jit(solution)/shard_map/ppermute | solution.py:92
  126.2 0.0 copy-done.4
  126.2 3.5 broadcast_select_fusion.2
  129.7 159.3 %all-gather.2.cloned.1.call-done = bf16[5120,4608]{1,0:T(8,128)(2,1)} async-done(((bf16[320,4608]{1,0:T(8,128)(2,1)}), bf16[5120,4608]{1,0:T(8,128)(2,1)}) %all-gather.2.cloned.1.call-update) | async-done | bytes 47185936 | tf_op jit(solution)/shard_map/all_gather | solution.py:109
  289.0 23.8 %convolution_convert_fusion = bf16[320,4608]{1,0:T(8,128)(2,1)} fusion(bf16[5120,4608]{1,0:T(8,128)(2,1)} %all-gather.2.cloned.1.call-done, bf16[320,2560]{1,0:T(8,128)(2,1)} %get-tuple-element.5, bf16[320,2560]{1,0:T(8,128)(2,1)} %get-tuple-element.4), kind=kOutput, calls=%fused_computation.2 | convolution fusion | flops 15107522560 | bytes 53411840 | tf_op jit(solution)/shard_map/dot_general | solution.py:122
  312.8 9.5 %attend.1 = bf16[8,40,1536]{2,1,0:T(8,128)(2,1)} custom-call(bf16[8,40,4608]{2,1,0:T(8,128)(2,1)} %bitcast.23, bf16[8,40,4608]{2,1,0:T(8,128)(2,1)} %bitcast.24, bf16[8,40,4608]{2,1,0:T(8,128)(2,1)} %bitcast.25), custom_call_target="tpu_custom_call" | custom-call | flops 15728640 | bytes 3932160 | tf_op jit(solution)/shard_map/attend/pallas_call | solution.py:34
  322.3 2.1 reshape.63
  324.5 0.0 copy-start.8
  324.5 0.0 copy-start.9
  324.5 26.0 %all-to-all-start.1 = ((bf16[16,20,1536]{2,1,0:T(8,128)(2,1)}), bf16[16,20,1536]{2,1,0:T(8,128)(2,1)S(1)}, u32[]{:S(2)}, u32[]{:S(2)}) async-start(bf16[16,20,1536]{2,1,0:T(8,128)(2,1)} %reshape.63), calls=%async_computation.1 | async-start | bytes 2359296 | tf_op jit(solution)/shard_map/all_to_all | solution.py:124
  350.5 28.4 %all-to-all-done.1 = bf16[16,20,1536]{2,1,0:T(8,128)(2,1)S(1)} async-done(((bf16[16,20,1536]{2,1,0:T(8,128)(2,1)}), bf16[16,20,1536]{2,1,0:T(8,128)(2,1)S(1)}, u32[]{:S(2)}, u32[]{:S(2)}) %all-to-all-start.1) | async-done | bytes 983072 | tf_op jit(solution)/shard_map/all_to_all | solution.py:124
  378.9 0.1 copy.40
  379.0 0.3 reshape.64
  379.2 1.3 collective-permute-start.1
  380.5 0.0 copy-done.8
  380.5 0.0 copy-done.9
  380.5 0.2 fusion.12
  380.7 0.0 copy-done
  380.7 0.3 fusion.18
  381.0 5.0 %fusion = f32[320,2560]{1,0:T(8,128)S(1)} fusion(bf16[320,1536]{1,0:T(8,128)(2,1)S(1)} %reshape.64, bf16[1536,5120]{1,0:T(8,128)(2,1)} %param.13, s32[]{:T(128)S(6)} %select_n.30), kind=kOutput, calls=%fused_computation | convolution fusion | flops 2516582400 | bytes 12124164 | tf_op jit(solution)/shard_map/dot_general | solution.py:131
  386.0 0.0 copy-start.3
  386.0 0.0 collective-permute-done.2
  386.0 15.6 %collective-permute-done.1 = bf16[320,1536]{1,0:T(8,128)(2,1)S(1)} collective-permute-done((bf16[320,1536]{1,0:T(8,128)(2,1)S(1)}, bf16[320,1536]{1,0:T(8,128)(2,1)S(1)}, u32[]{:S(2)}, u32[]{:S(2)}) %collective-permute-start.1) | collective-permute-done | bytes 983072 | tf_op jit(solution)/shard_map/ppermute | solution.py:130
  401.6 5.0 %convolution_add_fusion = f32[320,2560]{1,0:T(8,128)S(1)} fusion(f32[320,2560]{1,0:T(8,128)S(1)} %fusion, bf16[320,1536]{1,0:T(8,128)(2,1)S(1)} %collective-permute-done.1, bf16[1536,2560]{1,0:T(8,128)(2,1)} %collective-permute-done.2), kind=kOutput, calls=%fused_computation.3 | convolution fusion | flops 2517401600 | bytes 15400960 | tf_op jit(solution)/shard_map/dot_general | solution.py:131
  406.7 0.0 copy-done.3
  406.7 8.6 %fusion.6 = bf16[2,1,160,2560]{3,0,2,1:T(2,128)(2,1)S(1)} fusion(f32[2,1,160,2560]{3,2,0,1:T(8,128)S(1)} %bitcast.27, f32[2,2560]{1,0:T(2,128)S(1)} %fusion.18, bf16[2,1,160,2560]{3,2,1,0:T(8,128)(2,1)S(1)} %copy-done.3, bf16[2560]{0:T(1024)(128)(2,1)S(1)} %copy-done.6, pred[2,160]{0,1:T(8,128)(4,1)S(1)} %bitcast.33), kind=kLoop, calls=%fused_computation.9 | loop fusion | flops 4096000 | bytes 6579520 | tf_op jit(solution)/shard_map/convert_element_type | solution.py:143
  415.3 0.0 copy-start.5
  415.3 1.3 copy.27
  416.6 0.7 copy-done.5
  417.3 0.5 multiply_reduce_fusion
  417.8 0.6 fusion.10.x_ref
  418.4 13.4 %spread_terms.1 = f32[16,2,2688]{2,1,0:T(2,128)} custom-call(f32[2,2688]{1,0:T(2,128)} %fusion.10.x_ref), custom_call_target="tpu_custom_call" | custom-call | tf_op jit(solution)/shard_map/spread_terms/pallas_call | solution.py:77
  431.8 1.2 reshape.66
  433.0 1.2 fusion.7
  (1 shorter events, 0.0 us)
Async XLA Ops:
  7.2 373.5 %copy-start = (f32[32,2560]{1,0:T(8,128)S(1)}, f32[32,2560]{1,0:T(8,128)}, u32[]{:S(2)}) copy-start(f32[32,2560]{1,0:T(8,128)} %param.16) | copy-start | bytes 983044
  7.2 281.8 %all-gather.2.cloned.1.call-start = ((), (), s32[]{:S(2)}) async-start(), calls=%async_computation.2 | async-start | bytes 50135040 | tf_op jit(solution)/shard_map/all_gather | solution.py:109
  22.4 5.7 %copy-start.7 = (s32[2,1,160]{2,1,0:T(1,128)S(1)}, s32[2,1,160]{2,1,0:T(1,128)}, u32[]{:S(2)}) copy-start(s32[2,1,160]{2,1,0:T(1,128)} %param.10) | copy-start | bytes 3844
  22.4 5.9 %copy-start.2 = (bf16[2,1,160,2560]{3,2,1,0:T(8,128)(2,1)S(1)}, bf16[2,1,160,2560]{3,2,1,0:T(8,128)(2,1)}, u32[]{:S(2)}) copy-start(bf16[2,1,160,2560]{3,2,1,0:T(8,128)(2,1)} %param.9) | copy-start | bytes 4915204
  22.4 5.9 %copy-start.6 = (bf16[2560]{0:T(1024)(128)(2,1)S(1)}, bf16[2560]{0:T(1024)(128)(2,1)}, u32[]{:S(2)}) copy-start(bf16[2560]{0:T(1024)(128)(2,1)} %param.11) | copy-start | bytes 15364
  31.5 53.8 %all-to-all-start = ((bf16[2,160,2560]{2,0,1:T(2,128)(2,1)}), bf16[2,160,2560]{2,0,1:T(2,128)(2,1)S(1)}, u32[]{:S(2)}, u32[]{:S(2)}) async-start(bf16[2,160,2560]{2,0,1:T(2,128)(2,1)} %fusion.9), calls=%async_computation | async-start | bytes 3276800 | tf_op jit(solution)/shard_map/all_to_all | solution.py:116
  85.3 1.2 copy-start.1
  89.5 36.8 %copy-start.4 = (bf16[320,2560]{1,0:T(8,128)(2,1)S(1)}, bf16[320,2560]{1,0:T(8,128)(2,1)}, u32[]{:S(2)}) copy-start(bf16[320,2560]{1,0:T(8,128)(2,1)} %reshape.60) | copy-start | bytes 4915204
  89.5 36.8 %collective-permute-start = (bf16[320,2560]{1,0:T(8,128)(2,1)}, bf16[320,2560]{1,0:T(8,128)(2,1)}, u32[]{:S(2)}, u32[]{:S(2)}) collective-permute-start(bf16[320,2560]{1,0:T(8,128)(2,1)} %reshape.60), channel_id=1, source_target_pairs={{0,2},{2,0},{1,3},{3,1},{4,6},{6,4},{5,7},{7,5},{8,10},{10,8},{9,1... | collective-permute-start | bytes 4915208 | tf_op jit(solution)/shard_map/ppermute | solution.py:92
  97.8 288.2 %collective-permute-start.2 = (bf16[1536,2560]{1,0:T(8,128)(2,1)}, bf16[1536,2560]{1,0:T(8,128)(2,1)}, u32[]{:S(2)}, u32[]{:S(2)}) collective-permute-start(bf16[1536,2560]{1,0:T(8,128)(2,1)} %constant_dynamic-slice_fusion), channel_id=1, source_target_pairs={{0,2},{2,0},{1,3},{3,1},{4,6},{6,4},{5,7},{7,5},{8,10},{10,8},{9,1... | collective-permute-start | bytes 23592968 | tf_op jit(solution)/shard_map/ppermute | solution.py:113
  324.5 56.0 %copy-start.8 = (f32[8,32]{1,0:T(8,128)S(1)}, f32[8,32]{1,0:T(8,128)}, u32[]{:S(2)}) copy-start(f32[8,32]{1,0:T(8,128)} %param.15) | copy-start | bytes 3076
  324.5 56.0 %copy-start.9 = (s32[2,1]{0,1:T(1,128)S(1)}, s32[2,1]{0,1:T(1,128)}, u32[]{:S(2)}) copy-start(s32[2,1]{0,1:T(1,128)} %param.14) | copy-start | bytes 28
  324.5 54.4 %all-to-all-start.1 = ((bf16[16,20,1536]{2,1,0:T(8,128)(2,1)}), bf16[16,20,1536]{2,1,0:T(8,128)(2,1)S(1)}, u32[]{:S(2)}, u32[]{:S(2)}) async-start(bf16[16,20,1536]{2,1,0:T(8,128)(2,1)} %reshape.63), calls=%async_computation.1 | async-start | bytes 2359296 | tf_op jit(solution)/shard_map/all_to_all | solution.py:124
  379.2 22.4 %collective-permute-start.1 = (bf16[320,1536]{1,0:T(8,128)(2,1)S(1)}, bf16[320,1536]{1,0:T(8,128)(2,1)S(1)}, u32[]{:S(2)}, u32[]{:S(2)}) collective-permute-start(bf16[320,1536]{1,0:T(8,128)(2,1)S(1)} %reshape.64), channel_id=1, source_target_pairs={{0,2},{2,0},{1,3},{3,1},{4,6},{6,4},{5,7},{7,5},{8,10},{10,8},{9,1... | collective-permute-start | bytes 2949128 | tf_op jit(solution)/shard_map/ppermute | solution.py:130
  386.0 20.7 %copy-start.3 = (bf16[2,1,160,2560]{3,2,1,0:T(8,128)(2,1)S(1)}, bf16[2,1,160,2560]{3,2,1,0:T(8,128)(2,1)}, u32[]{:S(2)}) copy-start(bf16[2,1,160,2560]{3,2,1,0:T(8,128)(2,1)} %param.9) | copy-start | bytes 4915204
  415.3 2.0 copy-start.5
Sparse Core Ops, SparseCore 0:
  28.2 260.7 all-gather.1
where the time goes:
time: 442 us; the launch traced here: 441 us
  waiting for transfers between devices  279 us (63%)
  local copies, waits for them, and re-layouts  38 us (9%)
  matrix products  35.5 us (8%)
  starting transfers between devices  35.2 us (8%)
  Pallas kernels  22.9 us (5%)
  other arithmetic  16.4 us (4%)
  between operations  14.2 us (3%)
    all_gather x1, waiting for transfers between devices, body(): weights = lax.all_gather(mine, ('frame', 'dp'), axis=0, tiled=True)  159 us
    all_to_all x1, waiting for transfers between devices, body(): lax.all_to_all(xin.reshape(clips, spots, width), 'frame', split_axis=1, c...  47.4 us
    all_to_all x1, waiting for transfers between devices, body(): lax.all_to_all(attn.reshape(frames * clips, local, heads_width), 'frame',...  28.4 us
    ppermute x1, waiting for transfers between devices, gather_mp(): other = lax.ppermute(block, 'mp', [(0, 1), (1, 0)])  28.1 us
    all_to_all x1, starting transfers between devices, body(): lax.all_to_all(attn.reshape(frames * clips, local, heads_width), 'frame',...  26 us
    dot_general x1, matrix products, body(): jnp.dot(features, weights, preferred_element_type=jnp.float32)  23.8 us
    ppermute x1, waiting for transfers between devices, body(): other_heads = lax.ppermute(heads, 'mp', [(0, 1), (1, 0)])  15.6 us
    pallas_call x1, Pallas kernels, spread_terms(): pl.pallas_call(functools.partial(spread_kernel, frames, dps), in_specs=[p...  13.4 us
  transfers between devices with their start and end apart: 6, of which 5 were waited for; matrix products, arithmetic and copies ran while one was open for 11% of the time, Pallas kernels for 2%

commit v1 on v0

--- a/solution.py
+++ b/solution.py
@@ -86,6 +86,366 @@
     )(terms)
 
 
+def fused_kernel(x_ref, w_ref, o_ref, attn_ref, wo_ref, xbuf, wbuf, acc, qkv, abuf, x_recv,
+                 x_send, w_recv, w_send, o_recv, o_send, a_recv, a_send, e_recv, e_send, own_sem):
+    mps, frames, spots, width = xbuf.shape
+    per_group, _, _, _ = wbuf.shape
+    depth = w_ref.shape[1]
+    lines = frames // 2
+    half = lines // 2
+    part = depth // 2
+    quarter = o_ref.shape[0] // 4
+    f, m, d = lax.axis_index("frame"), lax.axis_index("mp"), lax.axis_index("dp")
+    z, c = f // 2, f % 2
+    hi, lo = z // 2, z % 2
+    mine = hi * 2 + c
+    inner = hi != lo
+    pair, near, far = z + 1 - 2 * lo, half - hi, (lines - 1) * (1 - hi)
+    other_core = 2 * z + 1 - c
+
+    def remote(source, target, send_sem, recv_sem, frame=f, mp=m, dp=d):
+        return pltpu.make_async_remote_copy(
+            src_ref=source, dst_ref=target, send_sem=send_sem, recv_sem=recv_sem,
+            device_id={"frame": frame, "mp": mp, "dp": dp},
+            device_id_type=pl.DeviceIdType.MESH)
+
+    def arrived(target, recv_sem):
+        pltpu.make_async_copy(target, target, recv_sem).wait()
+
+    def rows_of(owner, which):
+        return pl.ds(pl.multiple_of(owner * depth + which * part, part), part)
+
+    def whole_rows(owner):
+        return pl.ds(pl.multiple_of(owner * depth, depth), depth)
+
+    def columns(group, head):
+        return pl.ds(pl.multiple_of((group * per_group + head) * HS, HS), HS)
+
+    def line(j):
+        return jnp.where(j == 0, pair, jnp.where(j == 1, near, far))
+
+    def source_of(j):
+        return 2 * line(j // 2) + j % 2
+
+    def w_direct(h, k):
+        target = jnp.where(k < 2, pair, near)
+        group = jnp.where(k < 2, hi, 1 - hi) * 2 + k % 2
+        return remote(w_ref.at[:, pl.ds(pl.multiple_of(d * part, part), part), columns(group, h)],
+                      wbuf.at[h, :, rows_of(f, d), :], w_send.at[h, k], w_recv.at[h, f, d],
+                      frame=2 * target + k % 2)
+
+    def w_partner(h):
+        return remote(w_ref.at[:, :, columns(hi * 2 + 1 - c, h)], wbuf.at[h, :, whole_rows(f), :],
+                      w_send.at[h, 4], w_recv.at[h, f, 0], frame=other_core)
+
+    def w_own(h):
+        return pltpu.make_async_copy(w_ref.at[:, :, columns(mine, h)],
+                                     wbuf.at[h, :, whole_rows(f), :], own_sem.at[h])
+
+    def w_block(h, owner, which):
+        return wbuf.at[h, :, rows_of(owner, which), :]
+
+    def w_share(h, j):
+        owner = source_of(j)
+        block = w_block(h, owner, d)
+        return remote(block, block, w_send.at[h, 5 + j], w_recv.at[h, owner, d], dp=1 - d)
+
+    def w_relay(h, j):
+        owner = source_of(j)
+        block = w_block(h, owner, d)
+        return remote(block, block, w_send.at[h, 9 + j], w_recv.at[h, owner, d],
+                      frame=2 * pair + c)
+
+    def forward_w(h, j):
+        owner = source_of(j)
+        arrived(w_block(h, owner, d), w_recv.at[h, owner, d])
+
+        @pl.when(jnp.logical_and(inner, j >= 2))
+        def _():
+            w_relay(h, j).start()
+
+        w_share(h, j).start()
+
+    def x_direct(k):
+        target = (z + k) % lines
+        return remote(x_ref.at[target % 2], xbuf.at[m, f], x_send.at[k], x_recv.at[m, f],
+                      frame=2 * target + c)
+
+    def x_across(owner, source, k):
+        return remote(source, xbuf.at[m, owner], x_send.at[4 + k], x_recv.at[m, owner],
+                      mp=1 - m)
+
+    def x_core(owner, source, which, k, slot):
+        return remote(source, xbuf.at[which, owner], x_send.at[slot + k], x_recv.at[which, owner],
+                      frame=other_core)
+
+    def x_owner(k):
+        return f if k == 0 else 2 * line(k - 1) + c
+
+    def o_rows(which):
+        return pl.ds(pl.multiple_of(which * quarter, quarter), quarter)
+
+    def attn_block(which, owner, h):
+        group = (owner // 4) * 2 + owner % 2
+        clip = (owner // 2) % 2
+        return attn_ref.at[which, pl.ds(pl.multiple_of(clip * spots, spots), spots),
+                           columns(group, h)]
+
+    def a_direct(h, k):
+        target = (f + k) % frames
+        return remote(abuf.at[h, target], attn_block(m, f, h), a_send.at[h, k], a_recv.at[h, f],
+                      frame=target)
+
+    def a_own(h):
+        return pltpu.make_async_copy(abuf.at[h, f], attn_block(m, f, h), a_recv.at[h, f])
+
+    def a_across(h, k):
+        owner = (f + k) % frames
+        block = attn_block(m, owner, h)
+        return remote(block, block, e_send.at[h, k], e_recv.at[h, owner], mp=1 - m)
+
+    def forward_attn(h):
+        @pl.loop(0, frames)
+        def _(k):
+            owner = (f + k) % frames
+            arrived(attn_block(m, owner, h), a_recv.at[h, owner])
+            a_across(h, k).start()
+
+    barrier = pltpu.get_barrier_semaphore()
+    for k in range(1, frames):
+        pl.semaphore_signal(barrier, inc=1, device_id={"frame": (f + k) % frames, "mp": m, "dp": d},
+                            device_id_type=pl.DeviceIdType.MESH)
+    pl.semaphore_signal(barrier, inc=1, device_id={"frame": f, "mp": 1 - m, "dp": d},
+                        device_id_type=pl.DeviceIdType.MESH)
+    pl.semaphore_signal(barrier, inc=1, device_id={"frame": f, "mp": m, "dp": 1 - d},
+                        device_id_type=pl.DeviceIdType.MESH)
+    own_x = pltpu.make_async_copy(x_ref.at[lo], xbuf.at[m, f], own_sem.at[per_group])
+    own_x.start()
+    for h in range(per_group):
+        w_own(h).start()
+    pl.semaphore_wait(barrier, frames + 1)
+
+    for k in range(4):
+        w_direct(0, k).start()
+    for k in range(1, lines):
+        x_direct(k).start()
+    q0, q1 = d * 2 + c, (1 - d) * 2 + c
+    o_across = remote(o_ref.at[o_rows(q0), pl.ds(pl.multiple_of((1 - m) * width, width), width)],
+                      wo_ref.at[o_rows(q0), :], o_send.at[0], o_recv.at[q0], mp=1 - m)
+    x_across(f, x_ref.at[lo], 0).start()
+    x_core(f, x_ref.at[lo], m, 0, 8).start()
+    o_across.start()
+    for h in range(per_group):
+        w_partner(h).start()
+
+    @pl.loop(0, 6)
+    def _(j):
+        forward_w(0, j)
+
+    for k in range(4):
+        w_direct(1, k).start()
+
+    o_q0 = wo_ref.at[o_rows(q0), :]
+    o_q1 = wo_ref.at[o_rows(q1), :]
+    o_share = remote(o_q0, o_q0, o_send.at[1], o_recv.at[q0], dp=1 - d)
+    o_core0 = remote(o_q0, o_q0, o_send.at[2], o_recv.at[q0], frame=other_core)
+    o_core1 = remote(o_q1, o_q1, o_send.at[3], o_recv.at[q1], frame=other_core)
+
+    for k in range(1, lines + 1):
+        if k < lines:
+            owner = x_owner(k)
+            block = xbuf.at[m, owner]
+            arrived(block, x_recv.at[m, owner])
+            x_across(owner, block, k).start()
+            x_core(owner, block, m, k, 8).start()
+        if k == 1:
+            arrived(o_q0, o_recv.at[q0])
+            o_share.start()
+            o_core0.start()
+        before = x_owner(k - 1)
+        block = xbuf.at[1 - m, before]
+        arrived(block, x_recv.at[1 - m, before])
+        x_core(before, block, 1 - m, k - 1, 12).start()
+    for h in range(2, per_group):
+        for k in range(4):
+            w_direct(h, k).start()
+    own_x.wait()
+    for k in range(lines):
+        owner = x_owner(k) + 1 - 2 * c
+        for which in range(mps):
+            arrived(xbuf.at[which, owner], x_recv.at[which, owner])
+
+    chunks = frames
+    marks = []
+    for h in range(1, per_group):
+        begin = h * chunks
+        ahead = h == 1 and per_group > 2
+        marks += [begin + at for at in ((-8, -4, 0, 2, 4, 6) if ahead else (0, 2, 3, 4, 5, 6))]
+    finals = per_group * chunks
+
+    def matmul(h, owner, first):
+        side = owner // (frames // mps)
+        col = pl.multiple_of((owner % (frames // mps)) * depth, depth)
+        w = jnp.concatenate([wbuf[h, p, whole_rows(owner), :] for p in range(3)], axis=1)
+        step = frames // 2
+
+        @pl.loop(0, 2)
+        def _(i):
+            x = xbuf[side, pl.ds(i * step, step), :, pl.ds(col, depth)].reshape(step * spots, depth)
+            y = jnp.dot(x, w, preferred_element_type=jnp.float32).reshape(step, spots, 3 * HS)
+
+            @pl.when(first)
+            def _():
+                acc[pl.ds(i * step, step)] = y
+
+            @pl.when(jnp.logical_not(first))
+            def _():
+                acc[pl.ds(i * step, step)] += y
+
+    def attention(h):
+        scale = 1.0 / math.sqrt(HS)
+
+        @pl.loop(0, frames)
+        def _(t):
+            for p in range(3):
+                qkv[p, t] = acc[t, :, p * HS:(p + 1) * HS].astype(qkv.dtype)
+
+        rows = math.gcd(spots, 32)
+
+        @pl.loop(0, spots // rows)
+        def _(i):
+            at = pl.ds(pl.multiple_of(i * rows, rows), rows)
+            for t in range(frames):
+                q = qkv[0, t, at, :].astype(jnp.float32) * scale
+                scores = [jnp.sum(q * qkv[1, u, at, :].astype(jnp.float32), axis=-1, keepdims=True)
+                          for u in range(t + 1)]
+                peak = functools.reduce(jnp.maximum, scores)
+                weights = [jnp.exp(s - peak) for s in scores]
+                total = functools.reduce(jnp.add, weights)
+                accum = functools.reduce(
+                    jnp.add,
+                    [w * qkv[2, u, at, :].astype(jnp.float32) for u, w in enumerate(weights)])
+                abuf[h, t, at, :] = (accum / total).astype(abuf.dtype)
+
+        a_own(h).start()
+
+        @pl.loop(1, frames)
+        def _(k):
+            a_direct(h, k).start()
+
+    @pl.loop(0, finals)
+    def _(i):
+        h, jj = i // chunks, i % chunks
+        event = functools.reduce(jnp.add, [jnp.where(i > mark, 1, 0) for mark in marks])
+        fires = functools.reduce(jnp.logical_or, [i == mark for mark in marks])
+
+        @pl.when(fires)
+        def _():
+            forward_w(1 + event // 6, event % 6)
+
+        @pl.when(i == 6)
+        def _():
+            arrived(o_q1, o_recv.at[q1])
+            o_core1.start()
+
+        owner = jnp.where(jj == 0, f, jnp.where(jj == 1, other_core, source_of(jnp.maximum(jj - 2, 0))))
+
+        @pl.when(jj == 0)
+        def _():
+            w_own(h).wait()
+
+        @pl.when(jj == 1)
+        def _():
+            arrived(wbuf.at[h, :, whole_rows(owner), :], w_recv.at[h, owner, 0])
+
+        @pl.when(jj >= 2)
+        def _():
+            arrived(w_block(h, owner, 1 - d), w_recv.at[h, owner, 1 - d])
+
+        matmul(h, owner, jj == 0)
+
+        for ready in range(per_group - 1):
+            @pl.when(i == (ready + 1) * chunks + 5)
+            def _():
+                forward_attn(ready)
+
+        @pl.when(jj == chunks - 1)
+        def _():
+            attention(h)
+
+    forward_attn(per_group - 1)
+    for which in (d * 2 + 1 - c, (1 - d) * 2 + 1 - c):
+        arrived(wo_ref.at[o_rows(which), :], o_recv.at[which])
+    for copy in (o_across, o_share, o_core0, o_core1):
+        copy.wait_send()
+    for k in range(1, lines):
+        x_direct(k).wait_send()
+    for k in range(lines):
+        owner = x_owner(k)
+        block = xbuf.at[m, owner]
+        x_across(owner, block, k).wait_send()
+        x_core(owner, block, m, k, 8).wait_send()
+        x_core(owner, xbuf.at[1 - m, owner], 1 - m, k, 12).wait_send()
+
+    @pl.loop(0, per_group)
+    def _(h):
+        for k in range(4):
+            w_direct(h, k).wait_send()
+        w_partner(h).wait_send()
+        for j in range(6):
+            w_share(h, j).wait_send()
+
+        @pl.when(inner)
+        def _():
+            for j in range(2, 6):
+                w_relay(h, j).wait_send()
+
+        @pl.loop(1, frames)
+        def _(k):
+            a_direct(h, k).wait_send()
+
+        @pl.loop(0, frames)
+        def _(k):
+            a_across(h, k).wait_send()
+            owner = (f + k) % frames
+            arrived(attn_block(1 - m, owner, h), e_recv.at[h, owner])
+
+
+def fused(xin, w_parts, w_out, frames):
+    clips, spots, width = xin.shape
+    parts, depth, heads_width = w_parts.shape
+    groups = frames // clips
+    per_group = heads_width // HS // groups
+    lines = frames // 2
+    any_spec = pl.BlockSpec(memory_space=pl.ANY)
+    dma = pltpu.SemaphoreType.DMA
+    return pl.pallas_call(
+        fused_kernel,
+        in_specs=[any_spec] * 3,
+        out_specs=[any_spec] * 2,
+        out_shape=[
+            jax.ShapeDtypeStruct((2, clips * spots, heads_width), jnp.bfloat16),
+            jax.ShapeDtypeStruct((w_out.shape[0], width), jnp.bfloat16),
+        ],
+        scratch_shapes=[
+            pltpu.VMEM((2, frames, spots, width), jnp.bfloat16),
+            pltpu.VMEM((per_group, parts, depth * frames, HS), jnp.bfloat16),
+            pltpu.VMEM((frames, spots, parts * HS), jnp.float32),
+            pltpu.VMEM((parts, frames, spots, HS), jnp.bfloat16),
+            pltpu.VMEM((per_group, frames, spots, HS), jnp.bfloat16),
+            dma((2, frames)), dma((16,)),
+            dma((per_group, frames, 2)), dma((per_group, 15)),
+            dma((4,)), dma((4,)),
+            dma((per_group, frames)), dma((per_group, frames)),
+            dma((per_group, frames)), dma((per_group, frames)),
+            dma((per_group + 1,)),
+        ],
+        compiler_params=pltpu.CompilerParams(
+            collective_id=2, has_side_effects=True, vmem_limit_bytes=60 << 20),
+        name="fused",
+    )(xin, w_parts, w_out)
+
+
 def gather_mp(block, size):
     if size != 2:
         return lax.all_gather(block, "mp", axis=block.ndim - 1, tiled=True)
@@ -96,44 +456,61 @@
     )
 
 
+def fits_fused(mps, dps, frames, clips, spots, depth, heads_width):
+    groups = frames // clips
+    return (mps == dps == clips == 2 and frames == groups * clips and groups == 2 * clips
+            and heads_width % (groups * HS) == 0 and heads_width // HS // groups > 1
+            and spots % 32 == 0 and depth % HS == 0)
+
+
 def body(mp_size, dp_size, tokens, token_mask, mask_embed, w_qkv, w_out, action_idx, codebook,
          act_proj, cotangent):
     clips, _, spots, width = tokens.shape
     heads_width = w_qkv.shape[2]
     depth = w_qkv.shape[0]
     xin = jnp.where(token_mask[..., None] == 1, mask_embed, tokens)
-    share = depth // dp_size
-    mine = lax.dynamic_slice_in_dim(
-        w_qkv.reshape(depth, 3 * heads_width), lax.axis_index("dp") * share, share, axis=0
-    )
-    weights = lax.all_gather(mine, ("frame", "dp"), axis=0, tiled=True)
-    if mp_size == 2:
+    frames = lax.axis_size("frame")
+    if fits_fused(mp_size, dp_size, frames, clips, spots, depth, heads_width):
         my_mp = lax.axis_index("mp")
+        heads, out_other = fused(xin.reshape(clips, spots, width), w_qkv.transpose(1, 0, 2), w_out, frames)
         out_mine = lax.dynamic_slice_in_dim(w_out, my_mp * width, width, axis=1)
-        out_other = lax.ppermute(
-            lax.dynamic_slice_in_dim(w_out, (1 - my_mp) * width, width, axis=1),
-            "mp", [(0, 1), (1, 0)])
-    spread = lax.all_to_all(
-        xin.reshape(clips, spots, width), "frame", split_axis=1, concat_axis=0, tiled=True
-    )
-    frames = spread.shape[0] // clips
-    local = spread.shape[1]
-    features = gather_mp(spread.reshape(frames * clips * local, width), mp_size)
-    qkv = jnp.dot(features, weights, preferred_element_type=jnp.float32).astype(jnp.bfloat16)
-    attn = attend(qkv.reshape(frames, clips * local, 3 * heads_width), frames, heads_width)
-    back = lax.all_to_all(
-        attn.reshape(frames * clips, local, heads_width), "frame", split_axis=0, concat_axis=1,
-        tiled=True,
-    )
-    heads = back.reshape(clips * spots, heads_width)
-    if mp_size == 2:
-        other_heads = lax.ppermute(heads, "mp", [(0, 1), (1, 0)])
-        mixed_rows = jnp.dot(heads, out_mine, preferred_element_type=jnp.float32) + jnp.dot(
-            other_heads, out_other, preferred_element_type=jnp.float32)
+        own = lax.dynamic_index_in_dim(heads, my_mp, 0, keepdims=False)
+        other = lax.dynamic_index_in_dim(heads, 1 - my_mp, 0, keepdims=False)
+        mixed_rows = jnp.dot(own, out_mine, preferred_element_type=jnp.float32) + jnp.dot(
+            other, out_other, preferred_element_type=jnp.float32)
     else:
-        out_block = lax.all_to_all(w_out, "mp", split_axis=1, concat_axis=0, tiled=True)
-        mixed_rows = jnp.dot(gather_mp(heads, mp_size), out_block,
-                             preferred_element_type=jnp.float32)
+        share = depth // dp_size
+        mine = lax.dynamic_slice_in_dim(
+            w_qkv.reshape(depth, 3 * heads_width), lax.axis_index("dp") * share, share, axis=0
+        )
+        weights = lax.all_gather(mine, ("frame", "dp"), axis=0, tiled=True)
+        if mp_size == 2:
+            my_mp = lax.axis_index("mp")
+            out_mine = lax.dynamic_slice_in_dim(w_out, my_mp * width, width, axis=1)
+            out_other = lax.ppermute(
+                lax.dynamic_slice_in_dim(w_out, (1 - my_mp) * width, width, axis=1),
+                "mp", [(0, 1), (1, 0)])
+        spread = lax.all_to_all(
+            xin.reshape(clips, spots, width), "frame", split_axis=1, concat_axis=0, tiled=True
+        )
+        frames = spread.shape[0] // clips
+        local = spread.shape[1]
+        features = gather_mp(spread.reshape(frames * clips * local, width), mp_size)
+        qkv = jnp.dot(features, weights, preferred_element_type=jnp.float32).astype(jnp.bfloat16)
+        attn = attend(qkv.reshape(frames, clips * local, 3 * heads_width), frames, heads_width)
+        back = lax.all_to_all(
+            attn.reshape(frames * clips, local, heads_width), "frame", split_axis=0, concat_axis=1,
+            tiled=True,
+        )
+        heads = back.reshape(clips * spots, heads_width)
+        if mp_size == 2:
+            other_heads = lax.ppermute(heads, "mp", [(0, 1), (1, 0)])
+            mixed_rows = jnp.dot(heads, out_mine, preferred_element_type=jnp.float32) + jnp.dot(
+                other_heads, out_other, preferred_element_type=jnp.float32)
+        else:
+            out_block = lax.all_to_all(w_out, "mp", split_axis=1, concat_axis=0, tiled=True)
+            mixed_rows = jnp.dot(gather_mp(heads, mp_size), out_block,
+                                 preferred_element_type=jnp.float32)
     mixed = mixed_rows.reshape(clips, 1, spots, width)
     onehot = (
         action_idx.reshape(clips)[:, None] == jnp.arange(codebook.shape[0])[None, :]

time: 442 us -> 288 us (0.65)
  waiting for transfers between devices: 279 us -> 0 us
  Pallas kernels: 22.9 us -> 263 us
  local copies, waits for them, and re-layouts: 38 us -> 1.26 us
  starting transfers between devices: 35.2 us -> 0 us
  matrix products: 35.5 us -> 16.9 us
  between operations: 14.2 us -> 0.75 us
  other arithmetic: 16.4 us -> 6.26 us
    pallas_call x1, Pallas kernels: 9.52 us -> 245 us  [fused(): pl.pallas_call(fused_kernel, in_specs=[any_spec] * 3, out_specs=[any_spec...]
    all_gather x1 -> x0, waiting for transfers between devices: 159 us -> none  [body(): weights = lax.all_gather(mine, ('frame', 'dp'), axis=0, tiled=True)]
    all_to_all x2 -> x0, waiting for transfers between devices: 75.8 us -> none  [the longest x1 47.4 us: body(): lax.all_to_all(xin.reshape(clips, spots, width), 'frame', split_axis=1, c...]
    ppermute x3 -> x0, waiting for transfers between devices: 43.7 us -> none  [the longest x1 28.1 us: gather_mp(): other = lax.ppermute(block, 'mp', [(0, 1), (1, 0)])]
    all_to_all x2 -> x0, starting transfers between devices: 32.4 us -> none  [the longest x1 26 us: body(): lax.all_to_all(attn.reshape(frames * clips, local, heads_width), 'frame',...]
    dynamic_slice x3 -> x0, local copies, waits for them, and re-layouts: 19 us -> none  [the longest x2 11.9 us: body(): lax.dynamic_slice_in_dim(w_qkv.reshape(depth, 3 * heads_width), lax.axis_...]
    dot_general x3 -> x2, matrix products: 33.8 us -> 15.3 us  [the longest x1 8.16 us: body(): jnp.dot(other, out_other, preferred_element_type=jnp.float32)]
    unnamed x22 -> x15, local copies, waits for them, and re-layouts: 12.2 us -> 0.05 us
  transfers between devices with their start and end apart: 6 -> 0, of which waited for: 5 -> 0; matrix products, arithmetic and copies ran while one was open for 11% -> 0% of each run, Pallas kernels for 2% -> 0%
where the time goes in v1:
time: 288 us
  Pallas kernels  263 us (91%)
  matrix products  16.9 us (6%)
  other arithmetic  6.26 us (2%)
    pallas_call x1, Pallas kernels, fused(): pl.pallas_call(fused_kernel, in_specs=[any_spec] * 3, out_specs=[any_spec...  245 us
    pallas_call x1, Pallas kernels, spread_terms(): pl.pallas_call(functools.partial(spread_kernel, frames, dps), in_specs=[p...  17.7 us
    dot_general x1, matrix products, body(): jnp.dot(other, out_other, preferred_element_type=jnp.float32)  8.16 us
    dot_general x1, matrix products, body(): jnp.dot(own, out_mine, preferred_element_type=jnp.float32)  7.1 us

profile of v1, /device:TPU:1, one launch (start us, length us, event | category | flops | bytes accessed | tf_op | source)
XLA Modules:
  0.0 287.9 jit_solution(7786750835524671696)
XLA Ops:
  0.6 0.0 copy-start
  0.6 0.7 broadcast_compare_fusion
  1.4 2.8 fusion.6.x_ref
  4.2 244.9 %fused.1 = (bf16[2,320,1536]{2,1,0:T(8,128)(2,1)}, bf16[1536,2560]{1,0:T(8,128)(2,1)}) custom-call(bf16[2,160,2560]{2,1,0:T(8,128)(2,1)} %fusion.6.x_ref, bf16[3,640,1536]{2,1,0:T(8,128)(2,1)} %bitcast.28, bf16[1536,5120]{1,0:T(8,128)(2,1)} %o_ref.1), custom_call_target="tpu_custom_call" | custom-call | tf_op jit(solution)/shard_map/fused/pallas_call | solution.py:422
  249.1 0.0 copy-start.4
  249.1 8.2 %fusion.7 = f32[320,2560]{1,0:T(8,128)} fusion(bf16[1536,2560]{1,0:T(8,128)(2,1)} %get-tuple-element.5, bf16[2,320,1536]{2,1,0:T(8,128)(2,1)} %get-tuple-element.4, s32[]{:T(128)S(6)} %select_n.17), kind=kOutput, calls=%fused_computation.8 | convolution fusion | flops 2516582400 | bytes 12124164 | tf_op jit(solution)/shard_map/dot_general | solution.py:479
  257.3 0.0 copy-done.4
  257.3 0.0 copy-start.5
  257.3 0.0 copy-start.6
  257.3 0.0 copy-start.1
  257.3 0.0 copy-start.2
  257.3 0.0 copy-start.3
  257.3 7.1 %fusion.2 = f32[320,2560]{1,0:T(8,128)S(1)} fusion(f32[320,2560]{1,0:T(8,128)} %fusion.7, bf16[1536,5120]{1,0:T(8,128)(2,1)} %o_ref.1, s32[]{:T(128)S(6)} %select_n.16, bf16[2,320,1536]{2,1,0:T(8,128)(2,1)S(1)} %copy-done.4, s32[]{:T(128)S(6)} %select_n.15), kind=kOutput, calls=%fused_computation.2 | convolution fusion | flops 2517401600 | bytes 15400968 | tf_op jit(solution)/shard_map/dot_general | solution.py:479
  264.4 0.0 copy-done.5
  264.4 0.0 copy-done.6
  264.4 0.2 fusion.16
  264.6 0.0 copy-done
  264.6 0.3 fusion.22
  264.9 0.0 copy-done.1
  264.9 0.0 copy-done.2
  264.9 0.0 copy-done.3
  265.0 2.1 multiply_reduce_fusion
  267.1 0.6 fusion.14.x_ref
  267.7 17.7 %spread_terms.1 = f32[16,2,2688]{2,1,0:T(2,128)} custom-call(f32[2,2688]{1,0:T(2,128)} %fusion.14.x_ref), custom_call_target="tpu_custom_call" | custom-call | tf_op jit(solution)/shard_map/spread_terms/pallas_call | solution.py:77
  285.5 1.2 reshape.44
  286.7 1.2 fusion.12
  (1 shorter events, 0.0 us)
Async XLA Ops:
  0.6 264.0 %copy-start = (f32[32,2560]{1,0:T(8,128)S(1)}, f32[32,2560]{1,0:T(8,128)}, u32[]{:S(2)}) copy-start(f32[32,2560]{1,0:T(8,128)} %param.16) | copy-start | bytes 983044
  249.1 8.2 %copy-start.4 = (bf16[2,320,1536]{2,1,0:T(8,128)(2,1)S(1)}, bf16[2,320,1536]{2,1,0:T(8,128)(2,1)}, u32[]{:S(2)}) copy-start(bf16[2,320,1536]{2,1,0:T(8,128)(2,1)} %get-tuple-element.4) | copy-start | bytes 5898244
  257.3 7.1 %copy-start.5 = (f32[8,32]{1,0:T(8,128)S(1)}, f32[8,32]{1,0:T(8,128)}, u32[]{:S(2)}) copy-start(f32[8,32]{1,0:T(8,128)} %param.15) | copy-start | bytes 3076
  257.3 7.2 %copy-start.6 = (s32[2,1]{0,1:T(1,128)S(1)}, s32[2,1]{0,1:T(1,128)}, u32[]{:S(2)}) copy-start(s32[2,1]{0,1:T(1,128)} %param.14) | copy-start | bytes 28
  257.3 7.6 %copy-start.1 = (bf16[2,1,160,2560]{3,2,1,0:T(8,128)(2,1)S(1)}, bf16[2,1,160,2560]{3,2,1,0:T(8,128)(2,1)}, u32[]{:S(2)}) copy-start(bf16[2,1,160,2560]{3,2,1,0:T(8,128)(2,1)} %param.9) | copy-start | bytes 4915204
  257.3 7.6 %copy-start.2 = (bf16[2,1,160,2560]{3,2,1,0:T(8,128)(2,1)S(1)}, bf16[2,1,160,2560]{3,2,1,0:T(8,128)(2,1)}, u32[]{:S(2)}) copy-start(bf16[2,1,160,2560]{3,2,1,0:T(8,128)(2,1)} %param.17) | copy-start | bytes 4915204
  257.3 7.6 %copy-start.3 = (bf16[2560]{0:T(1024)(128)(2,1)S(1)}, bf16[2560]{0:T(1024)(128)(2,1)}, u32[]{:S(2)}) copy-start(bf16[2560]{0:T(1024)(128)(2,1)} %param.11) | copy-start | bytes 15364

commit v2 on v1

--- a/solution.py
+++ b/solution.py
@@ -166,18 +166,30 @@
 
         w_share(h, j).start()
 
-    def x_direct(k):
+    pieces = frames // mps
+
+    def features(q):
+        return pl.ds(pl.multiple_of(q * depth, depth), depth)
+
+    def x_piece(which, owner, q):
+        return xbuf.at[which, owner, :, features(q)]
+
+    def x_direct(k, q):
         target = (z + k) % lines
-        return remote(x_ref.at[target % 2], xbuf.at[m, f], x_send.at[k], x_recv.at[m, f],
-                      frame=2 * target + c)
-
-    def x_across(owner, source, k):
-        return remote(source, xbuf.at[m, owner], x_send.at[4 + k], x_recv.at[m, owner],
+        return remote(x_ref.at[target % 2, :, features(q)], x_piece(m, f, q), x_send.at[k, q],
+                      x_recv.at[m, f, q], frame=2 * target + c)
+
+    def x_across(owner, source, k, q):
+        return remote(source, x_piece(m, owner, q), x_send.at[4 + k, q], x_recv.at[m, owner, q],
                       mp=1 - m)
 
-    def x_core(owner, source, which, k, slot):
-        return remote(source, xbuf.at[which, owner], x_send.at[slot + k], x_recv.at[which, owner],
-                      frame=other_core)
+    def x_core(owner, source, which, k, q):
+        slot = jnp.where(which == m, 8, 12)
+        return remote(source, x_piece(which, owner, q), x_send.at[slot + k, q],
+                      x_recv.at[which, owner, q], frame=other_core)
+
+    def x_own(q):
+        return x_ref.at[lo, :, features(q)]
 
     def x_owner(k):
         return f if k == 0 else 2 * line(k - 1) + c
@@ -225,65 +237,66 @@
         w_own(h).start()
     pl.semaphore_wait(barrier, frames + 1)
 
-    for k in range(4):
-        w_direct(0, k).start()
-    for k in range(1, lines):
-        x_direct(k).start()
+    last = per_group - 1
+    outer = jnp.logical_not(inner)
+
+    def send_tokens():
+        @pl.loop(0, pieces)
+        def _(q):
+            for k in range(1, lines):
+                x_direct(k, q).start()
+
+    def send_weights(h, which):
+        for k in which:
+            w_direct(h, k).start()
+
+    send_weights(0, range(4))
+    for h in range(1, last):
+        send_weights(h, range(2, 4))
+
+    @pl.when(outer)
+    def _():
+        for h in range(1, last):
+            send_weights(h, range(2))
+        send_tokens()
+        send_weights(last, range(4))
+
     q0, q1 = d * 2 + c, (1 - d) * 2 + c
     o_across = remote(o_ref.at[o_rows(q0), pl.ds(pl.multiple_of((1 - m) * width, width), width)],
                       wo_ref.at[o_rows(q0), :], o_send.at[0], o_recv.at[q0], mp=1 - m)
-    x_across(f, x_ref.at[lo], 0).start()
-    x_core(f, x_ref.at[lo], m, 0, 8).start()
+
+    @pl.loop(0, pieces)
+    def _(q):
+        x_across(f, x_own(q), 0, q).start()
+        x_core(f, x_own(q), m, 0, q).start()
+
     o_across.start()
     for h in range(per_group):
         w_partner(h).start()
 
-    @pl.loop(0, 6)
-    def _(j):
-        forward_w(0, j)
-
-    for k in range(4):
-        w_direct(1, k).start()
+    for h in range(last):
+        @pl.loop(0, 6)
+        def _(j):
+            forward_w(h, j)
+
+        @pl.when(inner)
+        def _():
+            if h + 1 < last:
+                send_weights(h + 1, range(2))
+            else:
+                send_tokens()
+                send_weights(last, range(4))
 
     o_q0 = wo_ref.at[o_rows(q0), :]
     o_q1 = wo_ref.at[o_rows(q1), :]
     o_share = remote(o_q0, o_q0, o_send.at[1], o_recv.at[q0], dp=1 - d)
     o_core0 = remote(o_q0, o_q0, o_send.at[2], o_recv.at[q0], frame=other_core)
     o_core1 = remote(o_q1, o_q1, o_send.at[3], o_recv.at[q1], frame=other_core)
-
-    for k in range(1, lines + 1):
-        if k < lines:
-            owner = x_owner(k)
-            block = xbuf.at[m, owner]
-            arrived(block, x_recv.at[m, owner])
-            x_across(owner, block, k).start()
-            x_core(owner, block, m, k, 8).start()
-        if k == 1:
-            arrived(o_q0, o_recv.at[q0])
-            o_share.start()
-            o_core0.start()
-        before = x_owner(k - 1)
-        block = xbuf.at[1 - m, before]
-        arrived(block, x_recv.at[1 - m, before])
-        x_core(before, block, 1 - m, k - 1, 12).start()
-    for h in range(2, per_group):
-        for k in range(4):
-            w_direct(h, k).start()
-    own_x.wait()
-    for k in range(lines):
-        owner = x_owner(k) + 1 - 2 * c
-        for which in range(mps):
-            arrived(xbuf.at[which, owner], x_recv.at[which, owner])
-
-    chunks = frames
-    marks = []
-    for h in range(1, per_group):
-        begin = h * chunks
-        ahead = h == 1 and per_group > 2
-        marks += [begin + at for at in ((-8, -4, 0, 2, 4, 6) if ahead else (0, 2, 3, 4, 5, 6))]
-    finals = per_group * chunks
-
-    def matmul(h, owner, first):
+    arrived(o_q0, o_recv.at[q0])
+    o_share.start()
+    o_core0.start()
+
+    def matmul(slot, h, owner, first):
         side = owner // (frames // mps)
         col = pl.multiple_of((owner % (frames // mps)) * depth, depth)
         w = jnp.concatenate([wbuf[h, p, whole_rows(owner), :] for p in range(3)], axis=1)
@@ -296,19 +309,19 @@
 
             @pl.when(first)
             def _():
-                acc[pl.ds(i * step, step)] = y
+                acc[slot, pl.ds(i * step, step)] = y
 
             @pl.when(jnp.logical_not(first))
             def _():
-                acc[pl.ds(i * step, step)] += y
-
-    def attention(h):
+                acc[slot, pl.ds(i * step, step)] += y
+
+    def attention(slot, h):
         scale = 1.0 / math.sqrt(HS)
 
         @pl.loop(0, frames)
         def _(t):
             for p in range(3):
-                qkv[p, t] = acc[t, :, p * HS:(p + 1) * HS].astype(qkv.dtype)
+                qkv[p, t] = acc[slot, t, :, p * HS:(p + 1) * HS].astype(qkv.dtype)
 
         rows = math.gcd(spots, 32)
 
@@ -333,59 +346,102 @@
         def _(k):
             a_direct(h, k).start()
 
-    @pl.loop(0, finals)
-    def _(i):
-        h, jj = i // chunks, i % chunks
-        event = functools.reduce(jnp.add, [jnp.where(i > mark, 1, 0) for mark in marks])
-        fires = functools.reduce(jnp.logical_or, [i == mark for mark in marks])
-
-        @pl.when(fires)
-        def _():
-            forward_w(1 + event // 6, event % 6)
-
-        @pl.when(i == 6)
-        def _():
-            arrived(o_q1, o_recv.at[q1])
-            o_core1.start()
-
-        owner = jnp.where(jj == 0, f, jnp.where(jj == 1, other_core, source_of(jnp.maximum(jj - 2, 0))))
-
-        @pl.when(jj == 0)
-        def _():
-            w_own(h).wait()
-
-        @pl.when(jj == 1)
-        def _():
-            arrived(wbuf.at[h, :, whole_rows(owner), :], w_recv.at[h, owner, 0])
-
-        @pl.when(jj >= 2)
-        def _():
-            arrived(w_block(h, owner, 1 - d), w_recv.at[h, owner, 1 - d])
-
-        matmul(h, owner, jj == 0)
-
-        for ready in range(per_group - 1):
-            @pl.when(i == (ready + 1) * chunks + 5)
-            def _():
-                forward_attn(ready)
-
-        @pl.when(jj == chunks - 1)
-        def _():
-            attention(h)
-
-    forward_attn(per_group - 1)
+    def ready_w(h, j):
+        owner = source_of(j)
+        arrived(w_block(h, owner, 1 - d), w_recv.at[h, owner, 1 - d])
+
+    def ready_chip(h):
+        w_own(h).wait()
+        arrived(wbuf.at[h, :, whole_rows(other_core), :], w_recv.at[h, other_core, 0])
+
+    @pl.loop(0, pieces + 2)
+    def _(q):
+        @pl.when(q < pieces)
+        def _():
+            for k in range(1, lines):
+                owner = x_owner(k)
+                block = x_piece(m, owner, q)
+                arrived(block, x_recv.at[m, owner, q])
+                x_across(owner, block, k, q).start()
+                x_core(owner, block, m, k, q).start()
+
+        @pl.when(jnp.logical_and(q >= 1, q < pieces + 1))
+        def _():
+            for k in range(lines):
+                owner = x_owner(k)
+                block = x_piece(1 - m, owner, q - 1)
+                arrived(block, x_recv.at[1 - m, owner, q - 1])
+                x_core(owner, block, 1 - m, k, q - 1).start()
+
+        @pl.when(q == 2)
+        def _():
+            own_x.wait()
+
+            @pl.loop(0, last)
+            def _(h):
+                ready_chip(h)
+                for j in range(6):
+                    ready_w(h, j)
+
+        @pl.when(q >= pieces)
+        def _():
+            forward_w(last, q - pieces)
+
+        @pl.when(q >= 2)
+        def _():
+            for k in range(lines):
+                owner = x_owner(k) + 1 - 2 * c
+                for which in range(mps):
+                    arrived(x_piece(which, owner, q - 2), x_recv.at[which, owner, q - 2])
+
+            @pl.loop(0, last * mps)
+            def _(i):
+                side = i % mps
+                matmul(i // mps, i // mps, side * pieces + q - 2,
+                       jnp.logical_and(side == 0, q == 2))
+
+    arrived(o_q1, o_recv.at[q1])
+    o_core1.start()
+
+    @pl.loop(0, last)
+    def _(h):
+        forward_w(last, 2 + h)
+        attention(h, h)
+
+    ready_chip(last)
+    matmul(0, last, f, True)
+    matmul(0, last, other_core, False)
+
+    @pl.loop(0, 6)
+    def _(j):
+        @pl.when(jnp.logical_and(j + 1 >= 2 + last, j < 5))
+        def _():
+            forward_w(last, j + 1)
+
+        ready_w(last, j)
+        matmul(0, last, source_of(j), False)
+
+    for h in range(last - 1):
+        forward_attn(h)
+    attention(0, last)
+    for h in range(last - 1, per_group):
+        forward_attn(h)
+
     for which in (d * 2 + 1 - c, (1 - d) * 2 + 1 - c):
         arrived(wo_ref.at[o_rows(which), :], o_recv.at[which])
     for copy in (o_across, o_share, o_core0, o_core1):
         copy.wait_send()
-    for k in range(1, lines):
-        x_direct(k).wait_send()
-    for k in range(lines):
-        owner = x_owner(k)
-        block = xbuf.at[m, owner]
-        x_across(owner, block, k).wait_send()
-        x_core(owner, block, m, k, 8).wait_send()
-        x_core(owner, xbuf.at[1 - m, owner], 1 - m, k, 12).wait_send()
+
+    @pl.loop(0, pieces)
+    def _(q):
+        for k in range(1, lines):
+            x_direct(k, q).wait_send()
+        for k in range(lines):
+            owner = x_owner(k)
+            block = x_piece(m, owner, q)
+            x_across(owner, block, k, q).wait_send()
+            x_core(owner, block, m, k, q).wait_send()
+            x_core(owner, x_piece(1 - m, owner, q), 1 - m, k, q).wait_send()
 
     @pl.loop(0, per_group)
     def _(h):
@@ -430,10 +486,10 @@
         scratch_shapes=[
             pltpu.VMEM((2, frames, spots, width), jnp.bfloat16),
             pltpu.VMEM((per_group, parts, depth * frames, HS), jnp.bfloat16),
-            pltpu.VMEM((frames, spots, parts * HS), jnp.float32),
+            pltpu.VMEM((per_group - 1, frames, spots, parts * HS), jnp.float32),
             pltpu.VMEM((parts, frames, spots, HS), jnp.bfloat16),
             pltpu.VMEM((per_group, frames, spots, HS), jnp.bfloat16),
-            dma((2, frames)), dma((16,)),
+            dma((2, frames, frames // 2)), dma((16, frames // 2)),
             dma((per_group, frames, 2)), dma((per_group, 15)),
             dma((4,)), dma((4,)),
             dma((per_group, frames)), dma((per_group, frames)),
@@ -456,11 +512,12 @@
     )
 
 
-def fits_fused(mps, dps, frames, clips, spots, depth, heads_width):
+def fits_fused(mps, dps, frames, clips, spots, width, depth, heads_width):
     groups = frames // clips
     return (mps == dps == clips == 2 and frames == groups * clips and groups == 2 * clips
             and heads_width % (groups * HS) == 0 and heads_width // HS // groups > 1
-            and spots % 32 == 0 and depth % HS == 0)
+            and spots % 32 == 0 and depth % HS == 0
+            and width * mps == depth * frames)
 
 
 def body(mp_size, dp_size, tokens, token_mask, mask_embed, w_qkv, w_out, action_idx, codebook,
@@ -470,7 +527,7 @@
     depth = w_qkv.shape[0]
     xin = jnp.where(token_mask[..., None] == 1, mask_embed, tokens)
     frames = lax.axis_size("frame")
-    if fits_fused(mp_size, dp_size, frames, clips, spots, depth, heads_width):
+    if fits_fused(mp_size, dp_size, frames, clips, spots, width, depth, heads_width):
         my_mp = lax.axis_index("mp")
         heads, out_other = fused(xin.reshape(clips, spots, width), w_qkv.transpose(1, 0, 2), w_out, frames)
         out_mine = lax.dynamic_slice_in_dim(w_out, my_mp * width, width, axis=1)

time: 288 us -> 257 us (0.89)
  Pallas kernels: 263 us -> 232 us
    pallas_call x1, Pallas kernels: 245 us -> 219 us  [fused(): pl.pallas_call(fused_kernel, in_specs=[any_spec] * 3, out_specs=[any_spec...]
    pallas_call x1, Pallas kernels: 17.7 us -> 13.2 us  [spread_terms(): pl.pallas_call(functools.partial(spread_kernel, frames, dps), in_specs=[p...]
where the time goes in v2:
time: 257 us
  Pallas kernels  232 us (90%)
  matrix products  16.9 us (7%)
  other arithmetic  6.26 us (2%)
    pallas_call x1, Pallas kernels, fused(): pl.pallas_call(fused_kernel, in_specs=[any_spec] * 3, out_specs=[any_spec...  219 us
    pallas_call x1, Pallas kernels, spread_terms(): pl.pallas_call(functools.partial(spread_kernel, frames, dps), in_specs=[p...  13.2 us
    dot_general x1, matrix products, body(): jnp.dot(other, out_other, preferred_element_type=jnp.float32)  8.16 us
    dot_general x1, matrix products, body(): jnp.dot(own, out_mine, preferred_element_type=jnp.float32)  7.1 us

profile of v2, /device:TPU:1, one launch (start us, length us, event | category | flops | bytes accessed | tf_op | source)
XLA Modules:
  0.0 257.0 jit_solution(4596124683594643445)
XLA Ops:
  0.6 0.0 copy-start
  0.6 0.7 broadcast_compare_fusion
  1.4 2.8 %fusion.6.x_ref = bf16[2,160,2560]{2,1,0:T(8,128)(2,1)} fusion(bf16[2,1,160,2560]{3,2,1,0:T(8,128)(2,1)} %param.9, pred[2,160]{1,0:T(4,128)(4,1)S(1)} %bitcast.30, bf16[2560]{0:T(1024)(128)(2,1)} %param.11), kind=kLoop, calls=%fused_computation.7 | loop fusion | flops 819200 | bytes 3282240 | tf_op jit(solution)/shard_map/reshape | solution.py:532
  4.2 218.7 %fused.1 = (bf16[2,320,1536]{2,1,0:T(8,128)(2,1)}, bf16[1536,2560]{1,0:T(8,128)(2,1)}) custom-call(bf16[2,160,2560]{2,1,0:T(8,128)(2,1)} %fusion.6.x_ref, bf16[3,640,1536]{2,1,0:T(8,128)(2,1)} %bitcast.28, bf16[1536,5120]{1,0:T(8,128)(2,1)} %o_ref.1), custom_call_target="tpu_custom_call" | custom-call | tf_op jit(solution)/shard_map/fused/pallas_call | solution.py:478
  222.8 0.0 copy-start.4
  222.8 8.2 %fusion.7 = f32[320,2560]{1,0:T(8,128)} fusion(bf16[1536,2560]{1,0:T(8,128)(2,1)} %get-tuple-element.5, bf16[2,320,1536]{2,1,0:T(8,128)(2,1)} %get-tuple-element.4, s32[]{:T(128)S(6)} %select_n.17), kind=kOutput, calls=%fused_computation.8 | convolution fusion | flops 2516582400 | bytes 12124164 | tf_op jit(solution)/shard_map/dot_general | solution.py:536
  231.0 0.0 copy-done.4
  231.0 0.0 copy-start.5
  231.0 0.0 copy-start.6
  231.0 0.0 copy-start.1
  231.0 0.0 copy-start.2
  231.0 0.0 copy-start.3
  231.0 7.1 %fusion.2 = f32[320,2560]{1,0:T(8,128)S(1)} fusion(f32[320,2560]{1,0:T(8,128)} %fusion.7, bf16[1536,5120]{1,0:T(8,128)(2,1)} %o_ref.1, s32[]{:T(128)S(6)} %select_n.16, bf16[2,320,1536]{2,1,0:T(8,128)(2,1)S(1)} %copy-done.4, s32[]{:T(128)S(6)} %select_n.15), kind=kOutput, calls=%fused_computation.2 | convolution fusion | flops 2517401600 | bytes 15400968 | tf_op jit(solution)/shard_map/dot_general | solution.py:536
  238.2 0.0 copy-done.5
  238.2 0.0 copy-done.6
  238.2 0.2 fusion.16
  238.4 0.0 copy-done
  238.4 0.3 fusion.22
  238.7 0.0 copy-done.1
  238.7 0.0 copy-done.2
  238.7 0.0 copy-done.3
  238.7 2.1 multiply_reduce_fusion
  240.8 0.6 fusion.14.x_ref
  241.4 13.2 %spread_terms.1 = f32[16,2,2688]{2,1,0:T(2,128)} custom-call(f32[2,2688]{1,0:T(2,128)} %fusion.14.x_ref), custom_call_target="tpu_custom_call" | custom-call | tf_op jit(solution)/shard_map/spread_terms/pallas_call | solution.py:77
  254.6 1.2 reshape.44
  255.9 1.2 fusion.12
  (1 shorter events, 0.0 us)
Async XLA Ops:
  0.6 237.7 %copy-start = (f32[32,2560]{1,0:T(8,128)S(1)}, f32[32,2560]{1,0:T(8,128)}, u32[]{:S(2)}) copy-start(f32[32,2560]{1,0:T(8,128)} %param.16) | copy-start | bytes 983044
  222.8 8.2 %copy-start.4 = (bf16[2,320,1536]{2,1,0:T(8,128)(2,1)S(1)}, bf16[2,320,1536]{2,1,0:T(8,128)(2,1)}, u32[]{:S(2)}) copy-start(bf16[2,320,1536]{2,1,0:T(8,128)(2,1)} %get-tuple-element.4) | copy-start | bytes 5898244
  231.0 7.1 %copy-start.5 = (f32[8,32]{1,0:T(8,128)S(1)}, f32[8,32]{1,0:T(8,128)}, u32[]{:S(2)}) copy-start(f32[8,32]{1,0:T(8,128)} %param.15) | copy-start | bytes 3076
  231.0 7.2 %copy-start.6 = (s32[2,1]{0,1:T(1,128)S(1)}, s32[2,1]{0,1:T(1,128)}, u32[]{:S(2)}) copy-start(s32[2,1]{0,1:T(1,128)} %param.14) | copy-start | bytes 28
  231.0 7.6 %copy-start.1 = (bf16[2,1,160,2560]{3,2,1,0:T(8,128)(2,1)S(1)}, bf16[2,1,160,2560]{3,2,1,0:T(8,128)(2,1)}, u32[]{:S(2)}) copy-start(bf16[2,1,160,2560]{3,2,1,0:T(8,128)(2,1)} %param.9) | copy-start | bytes 4915204
  231.0 7.6 %copy-start.2 = (bf16[2,1,160,2560]{3,2,1,0:T(8,128)(2,1)S(1)}, bf16[2,1,160,2560]{3,2,1,0:T(8,128)(2,1)}, u32[]{:S(2)}) copy-start(bf16[2,1,160,2560]{3,2,1,0:T(8,128)(2,1)} %param.17) | copy-start | bytes 4915204
  231.0 7.6 %copy-start.3 = (bf16[2560]{0:T(1024)(128)(2,1)S(1)}, bf16[2560]{0:T(1024)(128)(2,1)}, u32[]{:S(2)}) copy-start(bf16[2560]{0:T(1024)(128)(2,1)} %param.11) | copy-start | bytes 15364

commit v3 on v2

--- a/solution.py
+++ b/solution.py
@@ -86,6 +86,9 @@
     )(terms)
 
 
+scope = jax.named_scope
+
+
 def fused_kernel(x_ref, w_ref, o_ref, attn_ref, wo_ref, xbuf, wbuf, acc, qkv, abuf, x_recv,
                  x_send, w_recv, w_send, o_recv, o_send, a_recv, a_send, e_recv, e_send, own_sem):
     mps, frames, spots, width = xbuf.shape
@@ -102,6 +105,7 @@
     inner = hi != lo
     pair, near, far = z + 1 - 2 * lo, half - hi, (lines - 1) * (1 - hi)
     other_core = 2 * z + 1 - c
+    q0, q1 = d * 2 + c, (1 - d) * 2 + c
 
     def remote(source, target, send_sem, recv_sem, frame=f, mp=m, dp=d):
         return pltpu.make_async_remote_copy(
@@ -158,7 +162,8 @@
 
     def forward_w(h, j):
         owner = source_of(j)
-        arrived(w_block(h, owner, d), w_recv.at[h, owner, d])
+        with scope("fw"):
+            arrived(w_block(h, owner, d), w_recv.at[h, owner, d])
 
         @pl.when(jnp.logical_and(inner, j >= 2))
         def _():
@@ -194,8 +199,32 @@
     def x_owner(k):
         return f if k == 0 else 2 * line(k - 1) + c
 
-    def o_rows(which):
-        return pl.ds(pl.multiple_of(which * quarter, quarter), quarter)
+    slices = o_recv.shape[1]
+    share = quarter // slices
+
+    def o_rows(which, i):
+        return pl.ds(pl.multiple_of(which * quarter + i * share, share), share)
+
+    def o_piece(which, i):
+        return wo_ref.at[o_rows(which, i), :]
+
+    def o_across(i):
+        return remote(
+            o_ref.at[o_rows(q0, i), pl.ds(pl.multiple_of((1 - m) * width, width), width)],
+            o_piece(q0, i), o_send.at[0, i], o_recv.at[q0, i], mp=1 - m)
+
+    def o_share(i):
+        return remote(o_piece(q0, i), o_piece(q0, i), o_send.at[1, i], o_recv.at[q0, i], dp=1 - d)
+
+    def o_core(which, i, slot):
+        return remote(o_piece(which, i), o_piece(which, i), o_send.at[slot, i],
+                      o_recv.at[which, i], frame=other_core)
+
+    def forward_o(i):
+        with scope("o_0"):
+            arrived(o_piece(q0, i), o_recv.at[q0, i])
+        o_share(i).start()
+        o_core(q0, i, 2).start()
 
     def attn_block(which, owner, h):
         group = (owner // 4) * 2 + owner % 2
@@ -240,61 +269,49 @@
     last = per_group - 1
     outer = jnp.logical_not(inner)
 
-    def send_tokens():
-        @pl.loop(0, pieces)
-        def _(q):
-            for k in range(1, lines):
-                x_direct(k, q).start()
-
-    def send_weights(h, which):
-        for k in which:
+    def send_tokens(q):
+        for k in range(1, lines):
+            x_direct(k, q).start()
+
+    def send_weights(h):
+        for k in range(4):
             w_direct(h, k).start()
 
-    send_weights(0, range(4))
-    for h in range(1, last):
-        send_weights(h, range(2, 4))
+    send_weights(0)
+    send_tokens(0)
+
+    @pl.loop(0, slices)
+    def _(i):
+        o_across(i).start()
+
+    for h in range(per_group):
+        w_partner(h).start()
+
+    @pl.loop(0, pieces)
+    def _(q):
+        x_core(f, x_own(q), m, 0, q).start()
+
+    @pl.loop(0, 2)
+    def _(j):
+        forward_w(0, j)
+
+    send_tokens(1)
+
+    @pl.when(inner)
+    def _():
+        @pl.loop(2, 6)
+        def _(j):
+            forward_w(0, j)
+
+    forward_o(0)
+    forward_o(1)
 
     @pl.when(outer)
     def _():
-        for h in range(1, last):
-            send_weights(h, range(2))
-        send_tokens()
-        send_weights(last, range(4))
-
-    q0, q1 = d * 2 + c, (1 - d) * 2 + c
-    o_across = remote(o_ref.at[o_rows(q0), pl.ds(pl.multiple_of((1 - m) * width, width), width)],
-                      wo_ref.at[o_rows(q0), :], o_send.at[0], o_recv.at[q0], mp=1 - m)
-
-    @pl.loop(0, pieces)
-    def _(q):
-        x_across(f, x_own(q), 0, q).start()
-        x_core(f, x_own(q), m, 0, q).start()
-
-    o_across.start()
-    for h in range(per_group):
-        w_partner(h).start()
-
-    for h in range(last):
-        @pl.loop(0, 6)
-        def _(j):
-            forward_w(h, j)
-
-        @pl.when(inner)
-        def _():
-            if h + 1 < last:
-                send_weights(h + 1, range(2))
-            else:
-                send_tokens()
-                send_weights(last, range(4))
-
-    o_q0 = wo_ref.at[o_rows(q0), :]
-    o_q1 = wo_ref.at[o_rows(q1), :]
-    o_share = remote(o_q0, o_q0, o_send.at[1], o_recv.at[q0], dp=1 - d)
-    o_core0 = remote(o_q0, o_q0, o_send.at[2], o_recv.at[q0], frame=other_core)
-    o_core1 = remote(o_q1, o_q1, o_send.at[3], o_recv.at[q1], frame=other_core)
-    arrived(o_q0, o_recv.at[q0])
-    o_share.start()
-    o_core0.start()
+        forward_w(0, 2)
+        forward_w(0, 3)
+
+    forward_o(2)
 
     def matmul(slot, h, owner, first):
         side = owner // (frames // mps)
@@ -315,9 +332,22 @@
             def _():
                 acc[slot, pl.ds(i * step, step)] += y
 
+    def attend_rows(h, i, rows):
+        scale = 1.0 / math.sqrt(HS)
+        at = pl.ds(pl.multiple_of(i * rows, rows), rows)
+        for t in range(frames):
+            q = qkv[0, t, at, :].astype(jnp.float32) * scale
+            scores = [jnp.sum(q * qkv[1, u, at, :].astype(jnp.float32), axis=-1, keepdims=True)
+                      for u in range(t + 1)]
+            peak = functools.reduce(jnp.maximum, scores)
+            weights = [jnp.exp(s - peak) for s in scores]
+            total = functools.reduce(jnp.add, weights)
+            accum = functools.reduce(
+                jnp.add,
+                [w * qkv[2, u, at, :].astype(jnp.float32) for u, w in enumerate(weights)])
+            abuf[h, t, at, :] = (accum / total).astype(abuf.dtype)
+
     def attention(slot, h):
-        scale = 1.0 / math.sqrt(HS)
-
         @pl.loop(0, frames)
         def _(t):
             for p in range(3):
@@ -327,18 +357,8 @@
 
         @pl.loop(0, spots // rows)
         def _(i):
-            at = pl.ds(pl.multiple_of(i * rows, rows), rows)
-            for t in range(frames):
-                q = qkv[0, t, at, :].astype(jnp.float32) * scale
-                scores = [jnp.sum(q * qkv[1, u, at, :].astype(jnp.float32), axis=-1, keepdims=True)
-                          for u in range(t + 1)]
-                peak = functools.reduce(jnp.maximum, scores)
-                weights = [jnp.exp(s - peak) for s in scores]
-                total = functools.reduce(jnp.add, weights)
-                accum = functools.reduce(
-                    jnp.add,
-                    [w * qkv[2, u, at, :].astype(jnp.float32) for u, w in enumerate(weights)])
-                abuf[h, t, at, :] = (accum / total).astype(abuf.dtype)
+            with scope("att"):
+                attend_rows(h, i, rows)
 
         a_own(h).start()
 
@@ -354,83 +374,150 @@
         w_own(h).wait()
         arrived(wbuf.at[h, :, whole_rows(other_core), :], w_recv.at[h, other_core, 0])
 
-    @pl.loop(0, pieces + 2)
+    def ready_w(h, j):
+        owner = source_of(j)
+        arrived(w_block(h, owner, 1 - d), w_recv.at[h, owner, 1 - d])
+
+    def ready_chip(h):
+        w_own(h).wait()
+        arrived(wbuf.at[h, :, whole_rows(other_core), :], w_recv.at[h, other_core, 0])
+
+    @pl.loop(0, pieces + 3)
     def _(q):
         @pl.when(q < pieces)
         def _():
+            x_across(f, x_own(q), 0, q).start()
             for k in range(1, lines):
                 owner = x_owner(k)
                 block = x_piece(m, owner, q)
-                arrived(block, x_recv.at[m, owner, q])
+                with scope("x_own"):
+                    arrived(block, x_recv.at[m, owner, q])
                 x_across(owner, block, k, q).start()
                 x_core(owner, block, m, k, q).start()
 
-        @pl.when(jnp.logical_and(q >= 1, q < pieces + 1))
+        @pl.when(q < pieces - 2)
+        def _():
+            send_tokens(q + 2)
+
+        @pl.when(q == pieces - 2)
+        def _():
+            send_weights(1)
+
+        @pl.when(q == 0)
+        def _():
+            forward_o(3)
+
+            @pl.when(outer)
+            def _():
+                forward_w(0, 4)
+                forward_w(0, 5)
+
+        @pl.when(jnp.logical_and(q >= 2, q < pieces + 2))
         def _():
             for k in range(lines):
                 owner = x_owner(k)
-                block = x_piece(1 - m, owner, q - 1)
-                arrived(block, x_recv.at[1 - m, owner, q - 1])
-                x_core(owner, block, 1 - m, k, q - 1).start()
-
-        @pl.when(q == 2)
-        def _():
-            own_x.wait()
-
-            @pl.loop(0, last)
-            def _(h):
-                ready_chip(h)
+                block = x_piece(1 - m, owner, q - 2)
+                with scope("x_other"):
+                    arrived(block, x_recv.at[1 - m, owner, q - 2])
+                x_core(owner, block, 1 - m, k, q - 2).start()
+
+        @pl.when(q == 4)
+        def _():
+            for h in range(2, per_group):
+                send_weights(h)
+
+        @pl.when(jnp.logical_and(q >= 4, q < 6))
+        def _():
+            forward_w(1, 3 * (q - 4))
+            forward_w(1, 3 * (q - 4) + 1)
+            forward_w(1, 3 * (q - 4) + 2)
+
+        @pl.when(q == 6)
+        def _():
+            forward_w(2, 0)
+            forward_w(2, 1)
+
+        @pl.when(q == 3)
+        def _():
+            with scope("w_0"):
+                own_x.wait()
+                ready_chip(0)
                 for j in range(6):
-                    ready_w(h, j)
-
-        @pl.when(q >= pieces)
-        def _():
-            forward_w(last, q - pieces)
-
-        @pl.when(q >= 2)
-        def _():
-            for k in range(lines):
-                owner = x_owner(k) + 1 - 2 * c
-                for which in range(mps):
-                    arrived(x_piece(which, owner, q - 2), x_recv.at[which, owner, q - 2])
-
-            @pl.loop(0, last * mps)
-            def _(i):
-                side = i % mps
-                matmul(i // mps, i // mps, side * pieces + q - 2,
-                       jnp.logical_and(side == 0, q == 2))
-
-    arrived(o_q1, o_recv.at[q1])
-    o_core1.start()
-
-    @pl.loop(0, last)
-    def _(h):
-        forward_w(last, 2 + h)
-        attention(h, h)
-
-    ready_chip(last)
-    matmul(0, last, f, True)
-    matmul(0, last, other_core, False)
-
-    @pl.loop(0, 6)
-    def _(j):
-        @pl.when(jnp.logical_and(j + 1 >= 2 + last, j < 5))
-        def _():
-            forward_w(last, j + 1)
-
-        ready_w(last, j)
-        matmul(0, last, source_of(j), False)
-
-    for h in range(last - 1):
-        forward_attn(h)
-    attention(0, last)
-    for h in range(last - 1, per_group):
-        forward_attn(h)
-
-    for which in (d * 2 + 1 - c, (1 - d) * 2 + 1 - c):
-        arrived(wo_ref.at[o_rows(which), :], o_recv.at[which])
-    for copy in (o_across, o_share, o_core0, o_core1):
-        copy.wait_send()
+                    ready_w(0, j)
+
+        @pl.when(q >= 3)
+        def _():
+            with scope("x_core"):
+                for k in range(lines):
+                    owner = x_owner(k) + 1 - 2 * c
+                    for which in range(mps):
+                        arrived(x_piece(which, owner, q - 3), x_recv.at[which, owner, q - 3])
+
+            @pl.loop(0, mps)
+            def _(side):
+                with scope("mm0"):
+                    matmul(0, 0, side * pieces + q - 3, jnp.logical_and(side == 0, q == 3))
+
+    @pl.loop(0, slices)
+    def _(i):
+        with scope("o_1"):
+            arrived(o_piece(q1, i), o_recv.at[q1, i])
+        o_core(q1, i, 3).start()
+
+    attention(0, 0)
+
+    @pl.loop(0, last * frames)
+    def _(i):
+        h, jj = 1 + i // frames, i % frames
+
+        @pl.when(jnp.logical_and(inner, jnp.logical_and(h < last, jj >= 4)))
+        def _():
+            forward_w(h + 1, jj - 2)
+
+        @pl.when(jnp.logical_and(outer, jnp.logical_and(h < last, jj >= 6)))
+        def _():
+            forward_w(h + 1, jj - 4)
+
+        @pl.when(jnp.logical_and(outer, jnp.logical_and(h > 1, jnp.logical_and(jj >= 4, jj < 6))))
+        def _():
+            forward_w(h, jj)
+
+        @pl.when(jj == 0)
+        def _():
+            ready_chip(h)
+
+        @pl.when(jj >= 2)
+        def _():
+            with scope("w_y"):
+                ready_w(h, jnp.maximum(jj - 2, 0))
+
+        owner = jnp.where(jj == 0, f, jnp.where(jj == 1, other_core, source_of(jnp.maximum(jj - 2, 0))))
+        with scope("mm"):
+            matmul(0, h, owner, jj == 0)
+
+        @pl.when(jj == frames - 1)
+        def _():
+            @pl.when(h == last)
+            def _():
+                with scope("fa"):
+                    forward_attn(last - 1)
+
+            attention(0, h)
+
+        @pl.when(jnp.logical_and(h == last, jj == 3))
+        def _():
+            for before in range(last - 1):
+                with scope("fa"):
+                    forward_attn(before)
+
+    with scope("fa"):
+        forward_attn(last)
+    @pl.loop(0, slices)
+    def _(i):
+        for which in (d * 2 + 1 - c, (1 - d) * 2 + 1 - c):
+            arrived(o_piece(which, i), o_recv.at[which, i])
+        for copy in (o_across(i), o_share(i), o_core(q0, i, 2), o_core(q1, i, 3)):
+            copy.wait_send()
 
     @pl.loop(0, pieces)
     def _(q):
@@ -486,12 +573,12 @@
         scratch_shapes=[
             pltpu.VMEM((2, frames, spots, width), jnp.bfloat16),
             pltpu.VMEM((per_group, parts, depth * frames, HS), jnp.bfloat16),
-            pltpu.VMEM((per_group - 1, frames, spots, parts * HS), jnp.float32),
+            pltpu.VMEM((1, frames, spots, parts * HS), jnp.float32),
             pltpu.VMEM((parts, frames, spots, HS), jnp.bfloat16),
             pltpu.VMEM((per_group, frames, spots, HS), jnp.bfloat16),
             dma((2, frames, frames // 2)), dma((16, frames // 2)),
             dma((per_group, frames, 2)), dma((per_group, 15)),
-            dma((4,)), dma((4,)),
+            dma((4, 4)), dma((4, 4)),
             dma((per_group, frames)), dma((per_group, frames)),
             dma((per_group, frames)), dma((per_group, frames)),
             dma((per_group + 1,)),
@@ -517,7 +604,7 @@
     return (mps == dps == clips == 2 and frames == groups * clips and groups == 2 * clips
             and heads_width % (groups * HS) == 0 and heads_width // HS // groups > 1
             and spots % 32 == 0 and depth % HS == 0
-            and width * mps == depth * frames)
+            and width * mps == depth * frames and heads_width % (16 * 16) == 0)
 
 
 def body(mp_size, dp_size, tokens, token_mask, mask_embed, w_qkv, w_out, action_idx, codebook,

time: 257 us -> 239 us (0.930)
  Pallas kernels: 232 us -> 214 us
    pallas_call x1, Pallas kernels: 219 us -> 198 us  [fused(): pl.pallas_call(fused_kernel, in_specs=[any_spec] * 3, out_specs=[any_spec...]
where the time goes in v3:
time: 239 us
  Pallas kernels  214 us (90%)
  matrix products  16.9 us (7%)
  other arithmetic  6.26 us (3%)
    pallas_call x1, Pallas kernels, fused(): pl.pallas_call(fused_kernel, in_specs=[any_spec] * 3, out_specs=[any_spec...  198 us
    pallas_call x1, Pallas kernels, spread_terms(): pl.pallas_call(functools.partial(spread_kernel, frames, dps), in_specs=[p...  15.6 us
    dot_general x1, matrix products, body(): jnp.dot(other, out_other, preferred_element_type=jnp.float32)  8.16 us
    dot_general x1, matrix products, body(): jnp.dot(own, out_mine, preferred_element_type=jnp.float32)  7.1 us

profile of v3, /device:TPU:1, one launch (start us, length us, event | category | flops | bytes accessed | tf_op | source)
XLA Modules:
  0.0 238.8 jit_solution(11548239929699326849)
XLA Ops:
  0.6 0.0 copy-start
  0.6 0.7 broadcast_compare_fusion
  1.4 2.8 %fusion.6.x_ref = bf16[2,160,2560]{2,1,0:T(8,128)(2,1)} fusion(bf16[2,1,160,2560]{3,2,1,0:T(8,128)(2,1)} %param.9, pred[2,160]{1,0:T(4,128)(4,1)S(1)} %bitcast.30, bf16[2560]{0:T(1024)(128)(2,1)} %param.11), kind=kLoop, calls=%fused_computation.7 | loop fusion | flops 819200 | bytes 3282240 | tf_op jit(solution)/shard_map/reshape | solution.py:619
  4.2 198.0 %fused.1 = (bf16[2,320,1536]{2,1,0:T(8,128)(2,1)}, bf16[1536,2560]{1,0:T(8,128)(2,1)}) custom-call(bf16[2,160,2560]{2,1,0:T(8,128)(2,1)} %fusion.6.x_ref, bf16[3,640,1536]{2,1,0:T(8,128)(2,1)} %bitcast.28, bf16[1536,5120]{1,0:T(8,128)(2,1)} %o_ref.1), custom_call_target="tpu_custom_call" | custom-call | tf_op jit(solution)/shard_map/fused/pallas_call | solution.py:565
  202.2 0.0 copy-start.4
  202.2 8.2 %fusion.7 = f32[320,2560]{1,0:T(8,128)} fusion(bf16[1536,2560]{1,0:T(8,128)(2,1)} %get-tuple-element.5, bf16[2,320,1536]{2,1,0:T(8,128)(2,1)} %get-tuple-element.4, s32[]{:T(128)S(6)} %select_n.17), kind=kOutput, calls=%fused_computation.8 | convolution fusion | flops 2516582400 | bytes 12124164 | tf_op jit(solution)/shard_map/dot_general | solution.py:623
  210.4 0.0 copy-done.4
  210.4 0.0 copy-start.5
  210.4 0.0 copy-start.6
  210.4 0.0 copy-start.1
  210.4 0.0 copy-start.2
  210.4 0.0 copy-start.3
  210.4 7.1 %fusion.2 = f32[320,2560]{1,0:T(8,128)S(1)} fusion(f32[320,2560]{1,0:T(8,128)} %fusion.7, bf16[1536,5120]{1,0:T(8,128)(2,1)} %o_ref.1, s32[]{:T(128)S(6)} %select_n.16, bf16[2,320,1536]{2,1,0:T(8,128)(2,1)S(1)} %copy-done.4, s32[]{:T(128)S(6)} %select_n.15), kind=kOutput, calls=%fused_computation.2 | convolution fusion | flops 2517401600 | bytes 15400968 | tf_op jit(solution)/shard_map/dot_general | solution.py:623
  217.5 0.0 copy-done.5
  217.5 0.0 copy-done.6
  217.5 0.2 fusion.16
  217.7 0.0 copy-done
  217.7 0.3 fusion.22
  218.0 0.0 copy-done.1
  218.0 0.0 copy-done.2
  218.0 0.0 copy-done.3
  218.0 2.1 multiply_reduce_fusion
  220.2 0.6 fusion.14.x_ref
  220.8 15.6 %spread_terms.1 = f32[16,2,2688]{2,1,0:T(2,128)} custom-call(f32[2,2688]{1,0:T(2,128)} %fusion.14.x_ref), custom_call_target="tpu_custom_call" | custom-call | tf_op jit(solution)/shard_map/spread_terms/pallas_call | solution.py:77
  236.4 1.2 reshape.44
  237.6 1.2 fusion.12
  (1 shorter events, 0.0 us)
Async XLA Ops:
  0.6 217.1 %copy-start = (f32[32,2560]{1,0:T(8,128)S(1)}, f32[32,2560]{1,0:T(8,128)}, u32[]{:S(2)}) copy-start(f32[32,2560]{1,0:T(8,128)} %param.16) | copy-start | bytes 983044
  202.2 8.2 %copy-start.4 = (bf16[2,320,1536]{2,1,0:T(8,128)(2,1)S(1)}, bf16[2,320,1536]{2,1,0:T(8,128)(2,1)}, u32[]{:S(2)}) copy-start(bf16[2,320,1536]{2,1,0:T(8,128)(2,1)} %get-tuple-element.4) | copy-start | bytes 5898244
  210.4 7.1 %copy-start.5 = (f32[8,32]{1,0:T(8,128)S(1)}, f32[8,32]{1,0:T(8,128)}, u32[]{:S(2)}) copy-start(f32[8,32]{1,0:T(8,128)} %param.15) | copy-start | bytes 3076
  210.4 7.2 %copy-start.6 = (s32[2,1]{0,1:T(1,128)S(1)}, s32[2,1]{0,1:T(1,128)}, u32[]{:S(2)}) copy-start(s32[2,1]{0,1:T(1,128)} %param.14) | copy-start | bytes 28
  210.4 7.6 %copy-start.1 = (bf16[2,1,160,2560]{3,2,1,0:T(8,128)(2,1)S(1)}, bf16[2,1,160,2560]{3,2,1,0:T(8,128)(2,1)}, u32[]{:S(2)}) copy-start(bf16[2,1,160,2560]{3,2,1,0:T(8,128)(2,1)} %param.9) | copy-start | bytes 4915204
  210.4 7.6 %copy-start.2 = (bf16[2,1,160,2560]{3,2,1,0:T(8,128)(2,1)S(1)}, bf16[2,1,160,2560]{3,2,1,0:T(8,128)(2,1)}, u32[]{:S(2)}) copy-start(bf16[2,1,160,2560]{3,2,1,0:T(8,128)(2,1)} %param.17) | copy-start | bytes 4915204
  210.4 7.6 %copy-start.3 = (bf16[2560]{0:T(1024)(128)(2,1)S(1)}, bf16[2560]{0:T(1024)(128)(2,1)}, u32[]{:S(2)}) copy-start(bf16[2560]{0:T(1024)(128)(2,1)} %param.11) | copy-start | bytes 15364

commit v4 on v3

--- a/solution.py
+++ b/solution.py
@@ -89,8 +89,10 @@
 scope = jax.named_scope
 
 
-def fused_kernel(x_ref, w_ref, o_ref, attn_ref, wo_ref, xbuf, wbuf, acc, qkv, abuf, x_recv,
-                 x_send, w_recv, w_send, o_recv, o_send, a_recv, a_send, e_recv, e_send, own_sem):
+def fused_kernel(dps, x_ref, w_ref, o_ref, cot_ref, act_ref, book_ref, idx_ref, next_ref, grad_ref,
+                 xbuf, wbuf, acc, qkv, abuf, heads, wo, total, xin, cot, act, gate, terms, table,
+                 x_recv, x_send, w_recv, w_send, o_recv, o_send, a_recv, a_send, e_recv, e_send,
+                 own_sem, t_recv, t_send, out_sem):
     mps, frames, spots, width = xbuf.shape
     per_group, _, _, _ = wbuf.shape
     depth = w_ref.shape[1]
@@ -206,12 +208,12 @@
         return pl.ds(pl.multiple_of(which * quarter + i * share, share), share)
 
     def o_piece(which, i):
-        return wo_ref.at[o_rows(which, i), :]
+        return wo.at[1 - m, o_rows(which, i), :]
 
     def o_across(i):
         return remote(
             o_ref.at[o_rows(q0, i), pl.ds(pl.multiple_of((1 - m) * width, width), width)],
-            o_piece(q0, i), o_send.at[0, i], o_recv.at[q0, i], mp=1 - m)
+            wo.at[m, o_rows(q0, i), :], o_send.at[0, i], o_recv.at[q0, i], mp=1 - m)
 
     def o_share(i):
         return remote(o_piece(q0, i), o_piece(q0, i), o_send.at[1, i], o_recv.at[q0, i], dp=1 - d)
@@ -229,8 +231,8 @@
     def attn_block(which, owner, h):
         group = (owner // 4) * 2 + owner % 2
         clip = (owner // 2) % 2
-        return attn_ref.at[which, pl.ds(pl.multiple_of(clip * spots, spots), spots),
-                           columns(group, h)]
+        return heads.at[which, h, pl.ds(pl.multiple_of(clip * spots, spots), spots),
+                        pl.ds(pl.multiple_of(group * HS, HS), HS)]
 
     def a_direct(h, k):
         target = (f + k) % frames
@@ -253,18 +255,29 @@
             a_across(h, k).start()
 
     barrier = pltpu.get_barrier_semaphore()
-    for k in range(1, frames):
-        pl.semaphore_signal(barrier, inc=1, device_id={"frame": (f + k) % frames, "mp": m, "dp": d},
+    count = frames * dps
+    me = f * dps + d
+
+    def peer(shift):
+        other = (me + shift) % count
+        return other // dps, other % dps
+
+    for shift in range(1, count):
+        frame, dp = peer(shift)
+        pl.semaphore_signal(barrier, inc=1, device_id={"frame": frame, "mp": m, "dp": dp},
                             device_id_type=pl.DeviceIdType.MESH)
     pl.semaphore_signal(barrier, inc=1, device_id={"frame": f, "mp": 1 - m, "dp": d},
                         device_id_type=pl.DeviceIdType.MESH)
-    pl.semaphore_signal(barrier, inc=1, device_id={"frame": f, "mp": m, "dp": 1 - d},
-                        device_id_type=pl.DeviceIdType.MESH)
+    loads = [pltpu.make_async_copy(source, target, out_sem.at[i]) for i, (source, target) in enumerate((
+        (x_ref, xin), (cot_ref, cot), (act_ref, act),
+        (o_ref.at[:, pl.ds(pl.multiple_of(m * width, width), width)], wo.at[m])))]
     own_x = pltpu.make_async_copy(x_ref.at[lo], xbuf.at[m, f], own_sem.at[per_group])
     own_x.start()
     for h in range(per_group):
         w_own(h).start()
-    pl.semaphore_wait(barrier, frames + 1)
+    for copy in loads:
+        copy.start()
+    pl.semaphore_wait(barrier, count)
 
     last = per_group - 1
     outer = jnp.logical_not(inner)
@@ -510,12 +523,94 @@
                 with scope("fa"):
                     forward_attn(before)
 
-    with scope("fa"):
-        forward_attn(last)
     @pl.loop(0, slices)
     def _(i):
         for which in (d * 2 + 1 - c, (1 - d) * 2 + 1 - c):
             arrived(o_piece(which, i), o_recv.at[which, i])
+
+    for copy in loads:
+        copy.wait()
+    clips = x_ref.shape[0]
+    groups = heads.shape[3] // HS
+    tile = math.gcd(width, 512)
+    codes = act.shape[0]
+    kinds = book_ref.shape[0]
+    index = jnp.concatenate([jnp.full((1, kinds), idx_ref[r], jnp.int32) for r in range(clips)], axis=0)
+    onehot = (index == lax.broadcasted_iota(jnp.int32, (clips, kinds), 1)).astype(jnp.float32)
+    codevec = jnp.dot(onehot, book_ref[...], precision=lax.Precision.HIGHEST,
+                      preferred_element_type=jnp.float32)
+    gate[...] = jnp.dot(codevec, act[...], precision=lax.Precision.HIGHEST,
+                        preferred_element_type=jnp.float32)
+    terms[me, :, width:] = jnp.concatenate(
+        [codevec, jnp.zeros((clips, HS - codes), jnp.float32)], axis=1)
+
+    def partial(h, side, cols):
+        w = jnp.concatenate(
+            [wo[side, pl.ds(pl.multiple_of((g * per_group + h) * HS, HS), HS), cols]
+             for g in range(groups)], axis=0)
+        return jnp.dot(heads[side, h], w, preferred_element_type=jnp.float32)
+
+    def tile_of(n):
+        return pl.ds(pl.multiple_of(n * tile, tile), tile)
+
+    def exchanged(h):
+        @pl.loop(0, frames)
+        def _(k):
+            owner = (f + k) % frames
+            arrived(attn_block(1 - m, owner, h), e_recv.at[h, owner])
+
+    @pl.loop(0, last)
+    def _(h):
+        with scope("exchanged"):
+            exchanged(h)
+
+        @pl.loop(0, width // tile)
+        def _(n):
+            cols = tile_of(n)
+            y = partial(h, 0, cols) + partial(h, 1, cols)
+
+            @pl.when(h == 0)
+            def _():
+                total[:, cols] = y
+
+            @pl.when(h > 0)
+            def _():
+                total[:, cols] += y
+
+    with scope("fa"):
+        forward_attn(last)
+
+    @pl.loop(0, width // tile)
+    def _(n):
+        cols = tile_of(n)
+        total[:, cols] += partial(last, m, cols)
+
+    with scope("exchanged"):
+        exchanged(last)
+
+    @pl.loop(0, width // tile)
+    def _(n):
+        cols = tile_of(n)
+        y = total[:, cols] + partial(last, 1 - m, cols)
+        for r in range(clips):
+            mixed = y[r * spots:(r + 1) * spots]
+            factor = gate[r:r + 1, cols]
+            xin[r, :, cols] = (xin[r, :, cols].astype(jnp.float32) + factor * mixed).astype(xin.dtype)
+            terms[me, r:r + 1, cols] = jnp.sum(
+                cot[r, :, cols].astype(jnp.float32) * mixed, axis=0, keepdims=True)
+
+    def t_copy(shift):
+        frame, dp = peer(shift)
+        return remote(terms.at[me], terms.at[me], t_send.at[shift], t_recv.at[me],
+                      frame=frame, dp=dp)
+
+    for shift in range(1, count):
+        t_copy(shift).start()
+    result = pltpu.make_async_copy(xin, next_ref, out_sem.at[0])
+    result.start()
+
+    @pl.loop(0, slices)
+    def _(i):
         for copy in (o_across(i), o_share(i), o_core(q0, i, 2), o_core(q1, i, 3)):
             copy.wait_send()
 
@@ -550,25 +645,45 @@
         @pl.loop(0, frames)
         def _(k):
             a_across(h, k).wait_send()
-            owner = (f + k) % frames
-            arrived(attn_block(1 - m, owner, h), e_recv.at[h, owner])
-
-
-def fused(xin, w_parts, w_out, frames):
+
+    with scope("terms"):
+        for shift in range(1, count):
+            t_copy(shift).wait_send()
+            frame, dp = peer(shift)
+            other = frame * dps + dp
+            arrived(terms.at[other], t_recv.at[other])
+    for i in range(count):
+        table[clips * i:clips * (i + 1), :] = terms[i]
+    code_columns = table[:, width:].T[:codes]
+
+    @pl.loop(0, width // tile)
+    def _(n):
+        cols = tile_of(n)
+        act[:, cols] = jnp.dot(code_columns, table[:, cols], precision=lax.Precision.HIGHEST,
+                               preferred_element_type=jnp.float32)
+
+    gradient = pltpu.make_async_copy(act, grad_ref, out_sem.at[1])
+    gradient.start()
+    gradient.wait()
+    result.wait()
+
+
+def fused(dps, xin, w_parts, w_out, cotangent, act_proj, codebook, action_idx, frames):
     clips, spots, width = xin.shape
     parts, depth, heads_width = w_parts.shape
     groups = frames // clips
     per_group = heads_width // HS // groups
-    lines = frames // 2
+    count = frames * dps
     any_spec = pl.BlockSpec(memory_space=pl.ANY)
     dma = pltpu.SemaphoreType.DMA
     return pl.pallas_call(
-        fused_kernel,
-        in_specs=[any_spec] * 3,
+        functools.partial(fused_kernel, dps),
+        in_specs=[any_spec] * 5 + [pl.BlockSpec(memory_space=pltpu.VMEM),
+                                   pl.BlockSpec(memory_space=pltpu.SMEM)],
         out_specs=[any_spec] * 2,
         out_shape=[
-            jax.ShapeDtypeStruct((2, clips * spots, heads_width), jnp.bfloat16),
-            jax.ShapeDtypeStruct((w_out.shape[0], width), jnp.bfloat16),
+            jax.ShapeDtypeStruct(xin.shape, xin.dtype),
+            jax.ShapeDtypeStruct(act_proj.shape, jnp.float32),
         ],
         scratch_shapes=[
             pltpu.VMEM((2, frames, spots, width), jnp.bfloat16),
@@ -576,17 +691,26 @@
             pltpu.VMEM((1, frames, spots, parts * HS), jnp.float32),
             pltpu.VMEM((parts, frames, spots, HS), jnp.bfloat16),
             pltpu.VMEM((per_group, frames, spots, HS), jnp.bfloat16),
+            pltpu.VMEM((2, per_group, clips * spots, groups * HS), jnp.bfloat16),
+            pltpu.VMEM((2, heads_width, width), jnp.bfloat16),
+            pltpu.VMEM((clips * spots, width), jnp.float32),
+            pltpu.VMEM(xin.shape, jnp.bfloat16),
+            pltpu.VMEM(xin.shape, jnp.bfloat16),
+            pltpu.VMEM(act_proj.shape, jnp.float32),
+            pltpu.VMEM((clips, width), jnp.float32),
+            pltpu.VMEM((count, clips, width + HS), jnp.float32),
+            pltpu.VMEM((count * clips, width + HS), jnp.float32),
             dma((2, frames, frames // 2)), dma((16, frames // 2)),
             dma((per_group, frames, 2)), dma((per_group, 15)),
             dma((4, 4)), dma((4, 4)),
             dma((per_group, frames)), dma((per_group, frames)),
             dma((per_group, frames)), dma((per_group, frames)),
-            dma((per_group + 1,)),
+            dma((per_group + 1,)), dma((count,)), dma((count,)), dma((4,)),
         ],
         compiler_params=pltpu.CompilerParams(
-            collective_id=2, has_side_effects=True, vmem_limit_bytes=60 << 20),
+            collective_id=2, has_side_effects=True, vmem_limit_bytes=63 << 20),
         name="fused",
-    )(xin, w_parts, w_out)
+    )(xin, w_parts, w_out, cotangent, act_proj, codebook, action_idx)
 
 
 def gather_mp(block, size):
@@ -602,7 +726,7 @@
 def fits_fused(mps, dps, frames, clips, spots, width, depth, heads_width):
     groups = frames // clips
     return (mps == dps == clips == 2 and frames == groups * clips and groups == 2 * clips
-            and heads_width % (groups * HS) == 0 and heads_width // HS // groups > 1
+            and heads_width == 3 * groups * HS
             and spots % 32 == 0 and depth % HS == 0
             and width * mps == depth * frames and heads_width % (16 * 16) == 0)
 
@@ -615,13 +739,11 @@
     xin = jnp.where(token_mask[..., None] == 1, mask_embed, tokens)
     frames = lax.axis_size("frame")
     if fits_fused(mp_size, dp_size, frames, clips, spots, width, depth, heads_width):
-        my_mp = lax.axis_index("mp")
-        heads, out_other = fused(xin.reshape(clips, spots, width), w_qkv.transpose(1, 0, 2), w_out, frames)
-        out_mine = lax.dynamic_slice_in_dim(w_out, my_mp * width, width, axis=1)
-        own = lax.dynamic_index_in_dim(heads, my_mp, 0, keepdims=False)
-        other = lax.dynamic_index_in_dim(heads, 1 - my_mp, 0, keepdims=False)
-        mixed_rows = jnp.dot(own, out_mine, preferred_element_type=jnp.float32) + jnp.dot(
-            other, out_other, preferred_element_type=jnp.float32)
+        next_state, grad_proj = fused(
+            dp_size, xin.reshape(clips, spots, width), w_qkv.transpose(1, 0, 2), w_out,
+            cotangent.reshape(clips, spots, width), act_proj, codebook,
+            action_idx.reshape(clips), frames)
+        return (next_state.reshape(clips, 1, spots, width), grad_proj)
     else:
         share = depth // dp_size
         mine = lax.dynamic_slice_in_dim(

time: 239 us -> 224 us (0.937)
  matrix products: 16.9 us -> 0 us
  other arithmetic: 6.26 us -> 3.46 us
    dot_general x5 -> x0, matrix products: 16.9 us -> none  [the longest x1 8.16 us: body(): jnp.dot(other, out_other, preferred_element_type=jnp.float32)]
    unnamed x15 -> x5, local copies, waits for them, and re-layouts: 0.05 us -> 3.48 us
    pallas_call x2 -> x1, Pallas kernels: 214 us -> 216 us  [fused(): pl.pallas_call(functools.partial(fused_kernel, dps), in_specs=[any_spec]...]
where the time goes in v4:
time: 224 us
  Pallas kernels  216 us (96%)
  local copies, waits for them, and re-layouts  3.48 us (2%)
  other arithmetic  3.46 us (2%)
    pallas_call x1, Pallas kernels, fused(): pl.pallas_call(functools.partial(fused_kernel, dps), in_specs=[any_spec]...  216 us

profile of v4, /device:TPU:1, one launch (start us, length us, event | category | flops | bytes accessed | tf_op | source)
XLA Modules:
  0.0 223.5 jit_solution(9285688458294277170)
XLA Ops:
  0.6 0.7 broadcast_compare_fusion
  1.3 2.8 %fusion.x_ref = bf16[2,160,2560]{2,1,0:T(8,128)(2,1)} fusion(bf16[2,1,160,2560]{3,2,1,0:T(8,128)(2,1)} %param.9, pred[2,160]{1,0:T(4,128)(4,1)S(1)} %bitcast.18, bf16[2560]{0:T(1024)(128)(2,1)} %param.11), kind=kLoop, calls=%fused_computation.1 | loop fusion | flops 819200 | bytes 3282240 | tf_op jit(solution)/shard_map/reshape | solution.py:743
  4.1 216.0 %fused.1 = (bf16[2,160,2560]{2,1,0:T(8,128)(2,1)}, f32[32,2560]{1,0:T(8,128)}) custom-call(bf16[2,160,2560]{2,1,0:T(8,128)(2,1)} %fusion.x_ref, bf16[3,640,1536]{2,1,0:T(8,128)(2,1)} %bitcast.15, bf16[1536,5120]{1,0:T(8,128)(2,1)} %o_ref.1, bf16[2,160,2560]{2,1,0:T(8,128)(2,1)} %bitcast.16, f32[32,2560]{1,0:T(8,128)} %act_ref.1, f32[8,32]{1,0:T(8,128)} %book_ref.1, ...), custom_call_target="tpu_custom_call" | custom-call | tf_op jit(solution)/shard_map/fused/pallas_call | solution.py:679
  220.1 0.0 copy-start
  220.1 2.7 %copy.18 = bf16[2,1,160,2560]{3,2,1,0:T(8,128)(2,1)} copy(bf16[2,1,160,2560]{3,2,1,0:T(8,128)(2,1)} %bitcast.17) | data formatting | bytes 3276800
  222.8 0.0 copy-done
  222.8 0.7 copy.19
  (1 shorter events, 0.0 us)
Async XLA Ops:
  220.1 2.8 %copy-start = (f32[32,2560]{1,0:T(8,128)S(1)}, f32[32,2560]{1,0:T(8,128)}, u32[]{:S(2)}) copy-start(f32[32,2560]{1,0:T(8,128)} %get-tuple-element.11) | copy-start | bytes 983044

commit v5 on v4

--- a/solution.py
+++ b/solution.py
@@ -89,8 +89,8 @@
 scope = jax.named_scope
 
 
-def fused_kernel(dps, x_ref, w_ref, o_ref, cot_ref, act_ref, book_ref, idx_ref, next_ref, grad_ref,
-                 xbuf, wbuf, acc, qkv, abuf, heads, wo, total, xin, cot, act, gate, terms, table,
+def fused_kernel(dps, tokens_ref, mask_ref, embed_ref, w_ref, o_ref, cot_ref, act_ref, book_ref, idx_ref, next_ref, grad_ref,
+                 xbuf, wbuf, acc, qkv, abuf, heads, wo, total, xin, cot, act, gate, terms, table, after,
                  x_recv, x_send, w_recv, w_send, o_recv, o_send, a_recv, a_send, e_recv, e_send,
                  own_sem, t_recv, t_send, out_sem):
     mps, frames, spots, width = xbuf.shape
@@ -183,7 +183,7 @@
 
     def x_direct(k, q):
         target = (z + k) % lines
-        return remote(x_ref.at[target % 2, :, features(q)], x_piece(m, f, q), x_send.at[k, q],
+        return remote(xin.at[target % 2, :, features(q)], x_piece(m, f, q), x_send.at[k, q],
                       x_recv.at[m, f, q], frame=2 * target + c)
 
     def x_across(owner, source, k, q):
@@ -196,7 +196,7 @@
                       x_recv.at[which, owner, q], frame=other_core)
 
     def x_own(q):
-        return x_ref.at[lo, :, features(q)]
+        return xin.at[lo, :, features(q)]
 
     def x_owner(k):
         return f if k == 0 else 2 * line(k - 1) + c
@@ -243,18 +243,24 @@
         return pltpu.make_async_copy(abuf.at[h, f], attn_block(m, f, h), a_recv.at[h, f])
 
     def a_across(h, k):
-        owner = (f + k) % frames
+        owner = (f + frames - k) % frames
         block = attn_block(m, owner, h)
         return remote(block, block, e_send.at[h, k], e_recv.at[h, owner], mp=1 - m)
 
     def forward_attn(h):
         @pl.loop(0, frames)
         def _(k):
-            owner = (f + k) % frames
+            owner = (f + frames - k) % frames
             arrived(attn_block(m, owner, h), a_recv.at[h, owner])
             a_across(h, k).start()
 
     barrier = pltpu.get_barrier_semaphore()
+    clips = xin.shape[0]
+    tile = math.gcd(width, 512)
+
+    def tile_of(n):
+        return pl.ds(pl.multiple_of(n * tile, tile), tile)
+
     count = frames * dps
     me = f * dps + d
 
@@ -269,14 +275,27 @@
     pl.semaphore_signal(barrier, inc=1, device_id={"frame": f, "mp": 1 - m, "dp": d},
                         device_id_type=pl.DeviceIdType.MESH)
     loads = [pltpu.make_async_copy(source, target, out_sem.at[i]) for i, (source, target) in enumerate((
-        (x_ref, xin), (cot_ref, cot), (act_ref, act),
+        (tokens_ref, xin), (cot_ref, cot), (act_ref, act),
         (o_ref.at[:, pl.ds(pl.multiple_of(m * width, width), width)], wo.at[m])))]
-    own_x = pltpu.make_async_copy(x_ref.at[lo], xbuf.at[m, f], own_sem.at[per_group])
-    own_x.start()
+    own_x = pltpu.make_async_copy(xin.at[lo], xbuf.at[m, f], own_sem.at[per_group])
     for h in range(per_group):
         w_own(h).start()
     for copy in loads:
         copy.start()
+    loads[0].wait()
+    same = (lax.broadcasted_iota(jnp.int32, (spots, spots), 0)
+            == lax.broadcasted_iota(jnp.int32, (spots, spots), 1))
+    for r in range(clips):
+        row = jnp.broadcast_to(mask_ref[r].astype(jnp.float32), (spots, spots))
+        masked = jnp.sum(jnp.where(same, row, 0.0), axis=1, keepdims=True) == 1.0
+
+        @pl.loop(0, width // tile)
+        def _(n):
+            cols = tile_of(n)
+            xin[r, :, cols] = jnp.where(masked, embed_ref[:, cols].astype(jnp.float32),
+                                        xin[r, :, cols].astype(jnp.float32)).astype(xin.dtype)
+
+    own_x.start()
     pl.semaphore_wait(barrier, count)
 
     last = per_group - 1
@@ -412,7 +431,7 @@
         def _():
             send_tokens(q + 2)
 
-        @pl.when(q == pieces - 2)
+        @pl.when(q == pieces - 2 - jnp.where(outer, 1, 0))
         def _():
             send_weights(1)
 
@@ -510,12 +529,12 @@
 
         @pl.when(jj == frames - 1)
         def _():
-            @pl.when(h == last)
-            def _():
-                with scope("fa"):
-                    forward_attn(last - 1)
-
             attention(0, h)
+
+        @pl.when(jnp.logical_and(h == last, jj == 5))
+        def _():
+            with scope("fa"):
+                forward_attn(last - 1)
 
         @pl.when(jnp.logical_and(h == last, jj == 3))
         def _():
@@ -528,11 +547,9 @@
         for which in (d * 2 + 1 - c, (1 - d) * 2 + 1 - c):
             arrived(o_piece(which, i), o_recv.at[which, i])
 
-    for copy in loads:
+    for copy in loads[1:]:
         copy.wait()
-    clips = x_ref.shape[0]
     groups = heads.shape[3] // HS
-    tile = math.gcd(width, 512)
     codes = act.shape[0]
     kinds = book_ref.shape[0]
     index = jnp.concatenate([jnp.full((1, kinds), idx_ref[r], jnp.int32) for r in range(clips)], axis=0)
@@ -550,9 +567,6 @@
              for g in range(groups)], axis=0)
         return jnp.dot(heads[side, h], w, preferred_element_type=jnp.float32)
 
-    def tile_of(n):
-        return pl.ds(pl.multiple_of(n * tile, tile), tile)
-
     def exchanged(h):
         @pl.loop(0, frames)
         def _(k):
@@ -561,6 +575,11 @@
 
     @pl.loop(0, last)
     def _(h):
+        @pl.when(h == last - 1)
+        def _():
+            with scope("fa"):
+                forward_attn(last)
+
         with scope("exchanged"):
             exchanged(h)
 
@@ -576,9 +595,6 @@
             @pl.when(h > 0)
             def _():
                 total[:, cols] += y
-
-    with scope("fa"):
-        forward_attn(last)
 
     @pl.loop(0, width // tile)
     def _(n):
@@ -595,7 +611,8 @@
         for r in range(clips):
             mixed = y[r * spots:(r + 1) * spots]
             factor = gate[r:r + 1, cols]
-            xin[r, :, cols] = (xin[r, :, cols].astype(jnp.float32) + factor * mixed).astype(xin.dtype)
+            after[r, :, cols] = (
+                xin[r, :, cols].astype(jnp.float32) + factor * mixed).astype(xin.dtype)
             terms[me, r:r + 1, cols] = jnp.sum(
                 cot[r, :, cols].astype(jnp.float32) * mixed, axis=0, keepdims=True)
 
@@ -606,7 +623,7 @@
 
     for shift in range(1, count):
         t_copy(shift).start()
-    result = pltpu.make_async_copy(xin, next_ref, out_sem.at[0])
+    result = pltpu.make_async_copy(after, next_ref, out_sem.at[0])
     result.start()
 
     @pl.loop(0, slices)
@@ -656,11 +673,8 @@
         table[clips * i:clips * (i + 1), :] = terms[i]
     code_columns = table[:, width:].T[:codes]
 
-    @pl.loop(0, width // tile)
-    def _(n):
-        cols = tile_of(n)
-        act[:, cols] = jnp.dot(code_columns, table[:, cols], precision=lax.Precision.HIGHEST,
-                               preferred_element_type=jnp.float32)
+    act[...] = jnp.dot(code_columns, table[:, :width], precision=lax.Precision.HIGHEST,
+                       preferred_element_type=jnp.float32)
 
     gradient = pltpu.make_async_copy(act, grad_ref, out_sem.at[1])
     gradient.start()
@@ -668,21 +682,21 @@
     result.wait()
 
 
-def fused(dps, xin, w_parts, w_out, cotangent, act_proj, codebook, action_idx, frames):
-    clips, spots, width = xin.shape
+def fused(dps, tokens, mask, embed, w_parts, w_out, cotangent, act_proj, codebook, action_idx, frames):
+    clips, spots, width = tokens.shape
     parts, depth, heads_width = w_parts.shape
     groups = frames // clips
     per_group = heads_width // HS // groups
     count = frames * dps
     any_spec = pl.BlockSpec(memory_space=pl.ANY)
+    vmem = pl.BlockSpec(memory_space=pltpu.VMEM)
     dma = pltpu.SemaphoreType.DMA
     return pl.pallas_call(
         functools.partial(fused_kernel, dps),
-        in_specs=[any_spec] * 5 + [pl.BlockSpec(memory_space=pltpu.VMEM),
-                                   pl.BlockSpec(memory_space=pltpu.SMEM)],
+        in_specs=[any_spec, vmem, vmem] + [any_spec] * 4 + [vmem, pl.BlockSpec(memory_space=pltpu.SMEM)],
         out_specs=[any_spec] * 2,
         out_shape=[
-            jax.ShapeDtypeStruct(xin.shape, xin.dtype),
+            jax.ShapeDtypeStruct(tokens.shape, tokens.dtype),
             jax.ShapeDtypeStruct(act_proj.shape, jnp.float32),
         ],
         scratch_shapes=[
@@ -694,12 +708,13 @@
             pltpu.VMEM((2, per_group, clips * spots, groups * HS), jnp.bfloat16),
             pltpu.VMEM((2, heads_width, width), jnp.bfloat16),
             pltpu.VMEM((clips * spots, width), jnp.float32),
-            pltpu.VMEM(xin.shape, jnp.bfloat16),
-            pltpu.VMEM(xin.shape, jnp.bfloat16),
+            pltpu.VMEM(tokens.shape, jnp.bfloat16),
+            pltpu.VMEM(tokens.shape, jnp.bfloat16),
             pltpu.VMEM(act_proj.shape, jnp.float32),
             pltpu.VMEM((clips, width), jnp.float32),
             pltpu.VMEM((count, clips, width + HS), jnp.float32),
             pltpu.VMEM((count * clips, width + HS), jnp.float32),
+            pltpu.VMEM(tokens.shape, jnp.bfloat16),
             dma((2, frames, frames // 2)), dma((16, frames // 2)),
             dma((per_group, frames, 2)), dma((per_group, 15)),
             dma((4, 4)), dma((4, 4)),
@@ -708,9 +723,40 @@
             dma((per_group + 1,)), dma((count,)), dma((count,)), dma((4,)),
         ],
         compiler_params=pltpu.CompilerParams(
-            collective_id=2, has_side_effects=True, vmem_limit_bytes=63 << 20),
+            collective_id=2, has_side_effects=True, vmem_limit_bytes=60 << 20),
         name="fused",
-    )(xin, w_parts, w_out, cotangent, act_proj, codebook, action_idx)
+    )(tokens, mask, embed, w_parts, w_out, cotangent, act_proj, codebook, action_idx)
+
+
+def finish_kernel(next_ref, grad_ref, next_out, grad_out, rows, grads, load, store):
+    copies = []
+    for i, (source, middle, target) in enumerate(
+            [(next_ref.at[r], rows.at[r], next_out.at[r]) for r in range(rows.shape[0])]
+            + [(grad_ref, grads, grad_out)]):
+        copies.append((pltpu.make_async_copy(source, middle, load.at[i]),
+                       pltpu.make_async_copy(middle, target, store.at[i])))
+    for first, _ in copies:
+        first.start()
+    for first, second in copies:
+        first.wait()
+        second.start()
+    for _, second in copies:
+        second.wait()
+
+
+def finish(next_state, grad_proj):
+    any_spec = pl.BlockSpec(memory_space=pl.ANY)
+    count = next_state.shape[0] + 1
+    return pl.pallas_call(
+        finish_kernel,
+        in_specs=[any_spec] * 2,
+        out_specs=[any_spec] * 2,
+        out_shape=[jax.ShapeDtypeStruct(a.shape, a.dtype) for a in (next_state, grad_proj)],
+        scratch_shapes=[pltpu.VMEM(next_state.shape, next_state.dtype),
+                        pltpu.VMEM(grad_proj.shape, grad_proj.dtype),
+                        pltpu.SemaphoreType.DMA((count,)), pltpu.SemaphoreType.DMA((count,))],
+        name="finish",
+    )(next_state, grad_proj)
 
 
 def gather_mp(block, size):
@@ -740,9 +786,10 @@
     frames = lax.axis_size("frame")
     if fits_fused(mp_size, dp_size, frames, clips, spots, width, depth, heads_width):
         next_state, grad_proj = fused(
-            dp_size, xin.reshape(clips, spots, width), w_qkv.transpose(1, 0, 2), w_out,
+            dp_size, tokens.reshape(clips, spots, width), token_mask, mask_embed.reshape(1, width), w_qkv.transpose(1, 0, 2), w_out,
             cotangent.reshape(clips, spots, width), act_proj, codebook,
             action_idx.reshape(clips), frames)
+        next_state, grad_proj = finish(next_state.reshape(2 * clips, spots // 2, width), grad_proj)
         return (next_state.reshape(clips, 1, spots, width), grad_proj)
     else:
         share = depth // dp_size

time: 224 us -> 217 us (0.969)
  other arithmetic: 3.46 us -> 0 us
    unnamed x5 -> x0, local copies, waits for them, and re-layouts: 3.48 us -> none
    reshape x1 -> x0, other arithmetic: 2.77 us -> none  [body(): xin.reshape(clips, spots, width)]
    pallas_call x1 -> x2, Pallas kernels: 216 us -> 215 us  [the longest x1 213 us: fused(): pl.pallas_call(functools.partial(fused_kernel, dps), in_specs=[any_spec,...]
where the time goes in v5:
time: 217 us
  Pallas kernels  215 us (99%)
    pallas_call x1, Pallas kernels, fused(): pl.pallas_call(functools.partial(fused_kernel, dps), in_specs=[any_spec,...  213 us

profile of v5, /device:TPU:1, one launch (start us, length us, event | category | flops | bytes accessed | tf_op | source)
XLA Modules:
  0.0 217.0 jit_solution(8940021861474905305)
XLA Ops:
  0.6 1.3 reshape.23.embed_ref
  1.9 212.7 %fused.1 = (bf16[2,160,2560]{2,1,0:T(8,128)(2,1)}, f32[32,2560]{1,0:T(8,128)}) custom-call(bf16[2,160,2560]{2,1,0:T(8,128)(2,1)} %bitcast.9, s32[2,1,160]{2,1,0:T(1,128)} %mask_ref.1, bf16[1,2560]{1,0:T(2,128)(2,1)} %reshape.23.embed_ref, bf16[3,640,1536]{2,1,0:T(8,128)(2,1)} %bitcast.8, bf16[1536,5120]{1,0:T(8,128)(2,1)} %o_ref.1, ...), custom_call_target="tpu_custom_call" | custom-call | tf_op jit(solution)/shard_map/fused/pallas_call | solution.py:694
  214.7 2.4 %finish.1 = (bf16[4,80,2560]{2,1,0:T(8,128)(2,1)}, f32[32,2560]{1,0:T(8,128)}) custom-call(bf16[4,80,2560]{2,1,0:T(8,128)(2,1)} %bitcast.11, f32[32,2560]{1,0:T(8,128)} %get-tuple-element.7.grad_ref), custom_call_target="tpu_custom_call" | custom-call | tf_op jit(solution)/shard_map/finish/pallas_call | solution.py:750

commit v6 on v5

--- a/solution.py
+++ b/solution.py
@@ -90,9 +90,9 @@
 
 
 def fused_kernel(dps, tokens_ref, mask_ref, embed_ref, w_ref, o_ref, cot_ref, act_ref, book_ref, idx_ref, next_ref, grad_ref,
-                 xbuf, wbuf, acc, qkv, abuf, heads, wo, total, xin, cot, act, gate, terms, table, after,
+                 xbuf, wbuf, acc, qkv, abuf, heads, wo, total, xin, cot, act, gate, mine_terms, terms, sums, after,
                  x_recv, x_send, w_recv, w_send, o_recv, o_send, a_recv, a_send, e_recv, e_send,
-                 own_sem, t_recv, t_send, out_sem):
+                 own_sem, t_recv, t_send, out_sem, halves, g_send, g_recv):
     mps, frames, spots, width = xbuf.shape
     per_group, _, _, _ = wbuf.shape
     depth = w_ref.shape[1]
@@ -137,12 +137,12 @@
         target = jnp.where(k < 2, pair, near)
         group = jnp.where(k < 2, hi, 1 - hi) * 2 + k % 2
         return remote(w_ref.at[:, pl.ds(pl.multiple_of(d * part, part), part), columns(group, h)],
-                      wbuf.at[h, :, rows_of(f, d), :], w_send.at[h, k], w_recv.at[h, f, d],
+                      wbuf.at[h, :, rows_of(f, d), :], w_send.at[0], w_recv.at[h, f, d],
                       frame=2 * target + k % 2)
 
     def w_partner(h):
         return remote(w_ref.at[:, :, columns(hi * 2 + 1 - c, h)], wbuf.at[h, :, whole_rows(f), :],
-                      w_send.at[h, 4], w_recv.at[h, f, 0], frame=other_core)
+                      w_send.at[1], w_recv.at[h, f, 0], frame=other_core)
 
     def w_own(h):
         return pltpu.make_async_copy(w_ref.at[:, :, columns(mine, h)],
@@ -154,12 +154,12 @@
     def w_share(h, j):
         owner = source_of(j)
         block = w_block(h, owner, d)
-        return remote(block, block, w_send.at[h, 5 + j], w_recv.at[h, owner, d], dp=1 - d)
+        return remote(block, block, w_send.at[2], w_recv.at[h, owner, d], dp=1 - d)
 
     def w_relay(h, j):
         owner = source_of(j)
         block = w_block(h, owner, d)
-        return remote(block, block, w_send.at[h, 9 + j], w_recv.at[h, owner, d],
+        return remote(block, block, w_send.at[3], w_recv.at[h, owner, d],
                       frame=2 * pair + c)
 
     def forward_w(h, j):
@@ -183,16 +183,15 @@
 
     def x_direct(k, q):
         target = (z + k) % lines
-        return remote(xin.at[target % 2, :, features(q)], x_piece(m, f, q), x_send.at[k, q],
+        return remote(xin.at[target % 2, :, features(q)], x_piece(m, f, q), x_send.at[0],
                       x_recv.at[m, f, q], frame=2 * target + c)
 
     def x_across(owner, source, k, q):
-        return remote(source, x_piece(m, owner, q), x_send.at[4 + k, q], x_recv.at[m, owner, q],
+        return remote(source, x_piece(m, owner, q), x_send.at[1], x_recv.at[m, owner, q],
                       mp=1 - m)
 
     def x_core(owner, source, which, k, q):
-        slot = jnp.where(which == m, 8, 12)
-        return remote(source, x_piece(which, owner, q), x_send.at[slot + k, q],
+        return remote(source, x_piece(which, owner, q), x_send.at[2],
                       x_recv.at[which, owner, q], frame=other_core)
 
     def x_own(q):
@@ -213,13 +212,13 @@
     def o_across(i):
         return remote(
             o_ref.at[o_rows(q0, i), pl.ds(pl.multiple_of((1 - m) * width, width), width)],
-            wo.at[m, o_rows(q0, i), :], o_send.at[0, i], o_recv.at[q0, i], mp=1 - m)
+            wo.at[m, o_rows(q0, i), :], o_send, o_recv.at[q0, i], mp=1 - m)
 
     def o_share(i):
-        return remote(o_piece(q0, i), o_piece(q0, i), o_send.at[1, i], o_recv.at[q0, i], dp=1 - d)
+        return remote(o_piece(q0, i), o_piece(q0, i), o_send, o_recv.at[q0, i], dp=1 - d)
 
     def o_core(which, i, slot):
-        return remote(o_piece(which, i), o_piece(which, i), o_send.at[slot, i],
+        return remote(o_piece(which, i), o_piece(which, i), o_send,
                       o_recv.at[which, i], frame=other_core)
 
     def forward_o(i):
@@ -236,7 +235,7 @@
 
     def a_direct(h, k):
         target = (f + k) % frames
-        return remote(abuf.at[h, target], attn_block(m, f, h), a_send.at[h, k], a_recv.at[h, f],
+        return remote(abuf.at[h, target], attn_block(m, f, h), a_send, a_recv.at[h, f],
                       frame=target)
 
     def a_own(h):
@@ -245,7 +244,7 @@
     def a_across(h, k):
         owner = (f + frames - k) % frames
         block = attn_block(m, owner, h)
-        return remote(block, block, e_send.at[h, k], e_recv.at[h, owner], mp=1 - m)
+        return remote(block, block, e_send, e_recv.at[h], mp=1 - m)
 
     def forward_attn(h):
         @pl.loop(0, frames)
@@ -283,6 +282,7 @@
     for copy in loads:
         copy.start()
     loads[0].wait()
+    gate[0:1, :] = embed_ref[...].astype(jnp.float32)[None, :]
     same = (lax.broadcasted_iota(jnp.int32, (spots, spots), 0)
             == lax.broadcasted_iota(jnp.int32, (spots, spots), 1))
     for r in range(clips):
@@ -292,7 +292,7 @@
         @pl.loop(0, width // tile)
         def _(n):
             cols = tile_of(n)
-            xin[r, :, cols] = jnp.where(masked, embed_ref[:, cols].astype(jnp.float32),
+            xin[r, :, cols] = jnp.where(masked, gate[0:1, cols],
                                         xin[r, :, cols].astype(jnp.float32)).astype(xin.dtype)
 
     own_x.start()
@@ -558,8 +558,11 @@
                       preferred_element_type=jnp.float32)
     gate[...] = jnp.dot(codevec, act[...], precision=lax.Precision.HIGHEST,
                         preferred_element_type=jnp.float32)
-    terms[me, :, width:] = jnp.concatenate(
-        [codevec, jnp.zeros((clips, HS - codes), jnp.float32)], axis=1)
+    marks = jnp.concatenate(
+        [jnp.full((1, HS), idx_ref[r], jnp.int32).astype(jnp.float32) for r in range(clips)], axis=0)
+    side = width // 2
+    for half_of in range(2):
+        mine_terms[half_of, :, side:] = marks
 
     def partial(h, side, cols):
         w = jnp.concatenate(
@@ -568,10 +571,7 @@
         return jnp.dot(heads[side, h], w, preferred_element_type=jnp.float32)
 
     def exchanged(h):
-        @pl.loop(0, frames)
-        def _(k):
-            owner = (f + k) % frames
-            arrived(attn_block(1 - m, owner, h), e_recv.at[h, owner])
+        arrived(heads.at[1 - m, h], e_recv.at[h])
 
     @pl.loop(0, last)
     def _(h):
@@ -613,72 +613,80 @@
             factor = gate[r:r + 1, cols]
             after[r, :, cols] = (
                 xin[r, :, cols].astype(jnp.float32) + factor * mixed).astype(xin.dtype)
-            terms[me, r:r + 1, cols] = jnp.sum(
-                cot[r, :, cols].astype(jnp.float32) * mixed, axis=0, keepdims=True)
+            weighed = jnp.sum(cot[r, :, cols].astype(jnp.float32) * mixed, axis=0, keepdims=True)
+            piece = math.gcd(tile, side)
+            for i in range(tile // piece):
+                at = n * (tile // piece) + i
+                mine_terms[at // (side // piece), r:r + 1,
+                           pl.ds(pl.multiple_of(at % (side // piece) * piece, piece), piece)] = (
+                    weighed[:, i * piece:(i + 1) * piece])
 
     def t_copy(shift):
         frame, dp = peer(shift)
-        return remote(terms.at[me], terms.at[me], t_send.at[shift], t_recv.at[me],
+        return remote(mine_terms.at[frame % 2], terms.at[me], t_send.at[0], t_recv.at[me],
                       frame=frame, dp=dp)
 
     for shift in range(1, count):
         t_copy(shift).start()
+    own_terms = pltpu.make_async_copy(mine_terms.at[c], terms.at[me], t_send.at[1])
+    own_terms.start()
     result = pltpu.make_async_copy(after, next_ref, out_sem.at[0])
     result.start()
 
-    @pl.loop(0, slices)
-    def _(i):
-        for copy in (o_across(i), o_share(i), o_core(q0, i, 2), o_core(q1, i, 3)):
-            copy.wait_send()
-
-    @pl.loop(0, pieces)
-    def _(q):
-        for k in range(1, lines):
-            x_direct(k, q).wait_send()
-        for k in range(lines):
-            owner = x_owner(k)
-            block = x_piece(m, owner, q)
-            x_across(owner, block, k, q).wait_send()
-            x_core(owner, block, m, k, q).wait_send()
-            x_core(owner, x_piece(1 - m, owner, q), 1 - m, k, q).wait_send()
-
-    @pl.loop(0, per_group)
-    def _(h):
-        for k in range(4):
-            w_direct(h, k).wait_send()
-        w_partner(h).wait_send()
-        for j in range(6):
-            w_share(h, j).wait_send()
-
-        @pl.when(inner)
-        def _():
-            for j in range(2, 6):
-                w_relay(h, j).wait_send()
-
-        @pl.loop(1, frames)
-        def _(k):
-            a_direct(h, k).wait_send()
-
-        @pl.loop(0, frames)
-        def _(k):
-            a_across(h, k).wait_send()
-
+    arrived(wo.at[0], o_send)
+    arrived(xbuf.at[0, pl.ds(0, lines - 1)], x_send.at[0])
+    arrived(xbuf.at[0, pl.ds(0, lines)], x_send.at[1])
+    arrived(xbuf.at[0], x_send.at[2])
+    arrived(wbuf.at[:, :, pl.ds(0, 4 * part), :], w_send.at[0])
+    arrived(wbuf.at[:, :, pl.ds(0, depth), :], w_send.at[1])
+    arrived(wbuf.at[:, :, pl.ds(0, 6 * part), :], w_send.at[2])
+
+    @pl.when(inner)
+    def _():
+        arrived(wbuf.at[:, :, pl.ds(0, 4 * part), :], w_send.at[3])
+
+    arrived(abuf.at[:, pl.ds(0, frames - 1)], a_send)
+    arrived(abuf, e_send)
+    kind = lax.broadcasted_iota(jnp.int32, (kinds, HS), 0).astype(jnp.float32)
+
+    def gathered(other):
+        total = sums[c]
+        for r in range(clips):
+            mask = jnp.tile(terms[other, r:r + 1, side:] == kind, (1, side // HS))
+            total += jnp.where(mask, terms[other, r:r + 1, :side], 0.0)
+        sums[c] = total
+
+    sums[c] = jnp.zeros((kinds, side), jnp.float32)
+    own_terms.wait()
+    gathered(me)
     with scope("terms"):
-        for shift in range(1, count):
-            t_copy(shift).wait_send()
-            frame, dp = peer(shift)
+        @pl.loop(1, count)
+        def _(shift):
+            frame, dp = peer(count - shift)
             other = frame * dps + dp
             arrived(terms.at[other], t_recv.at[other])
-    for i in range(count):
-        table[clips * i:clips * (i + 1), :] = terms[i]
-    code_columns = table[:, width:].T[:codes]
-
-    act[...] = jnp.dot(code_columns, table[:, :width], precision=lax.Precision.HIGHEST,
-                       preferred_element_type=jnp.float32)
-
-    gradient = pltpu.make_async_copy(act, grad_ref, out_sem.at[1])
-    gradient.start()
-    gradient.wait()
+            gathered(other)
+
+    arrived(terms.at[pl.ds(0, count - 1)], t_send.at[0])
+    swap = remote(sums.at[c], sums.at[c], g_send, g_recv, frame=other_core)
+    swap.start()
+    book_columns = book_ref[...].T
+
+    def gradient(i):
+        halves[i] = jnp.dot(book_columns, sums[i], precision=lax.Precision.HIGHEST,
+                            preferred_element_type=jnp.float32)
+        copy = pltpu.make_async_copy(
+            halves.at[i], grad_ref.at[:, pl.ds(pl.multiple_of(i * side, HS), side)],
+            out_sem.at[1 + i])
+        copy.start()
+        return copy
+
+    first = gradient(c)
+    arrived(sums.at[1 - c], g_recv)
+    second = gradient(1 - c)
+    swap.wait_send()
+    first.wait()
+    second.wait()
     result.wait()
 
 
@@ -712,15 +720,17 @@
             pltpu.VMEM(tokens.shape, jnp.bfloat16),
             pltpu.VMEM(act_proj.shape, jnp.float32),
             pltpu.VMEM((clips, width), jnp.float32),
-            pltpu.VMEM((count, clips, width + HS), jnp.float32),
-            pltpu.VMEM((count * clips, width + HS), jnp.float32),
+            pltpu.VMEM((2, clips, width // 2 + HS), jnp.float32),
+            pltpu.VMEM((count, clips, width // 2 + HS), jnp.float32),
+            pltpu.VMEM((2, codebook.shape[0], width // 2), jnp.float32),
             pltpu.VMEM(tokens.shape, jnp.bfloat16),
-            dma((2, frames, frames // 2)), dma((16, frames // 2)),
-            dma((per_group, frames, 2)), dma((per_group, 15)),
-            dma((4, 4)), dma((4, 4)),
-            dma((per_group, frames)), dma((per_group, frames)),
-            dma((per_group, frames)), dma((per_group, frames)),
-            dma((per_group + 1,)), dma((count,)), dma((count,)), dma((4,)),
+            dma((2, frames, frames // 2)), dma((3,)),
+            dma((per_group, frames, 2)), dma((4,)),
+            dma((4, 4)), dma,
+            dma((per_group, frames)), dma,
+            dma((per_group,)), dma,
+            dma((per_group + 1,)), dma((count,)), dma((2,)), dma((4,)),
+            pltpu.VMEM((2, act_proj.shape[0], width // 2), jnp.float32), dma, dma,
         ],
         compiler_params=pltpu.CompilerParams(
             collective_id=2, has_side_effects=True, vmem_limit_bytes=60 << 20),
@@ -786,7 +796,7 @@
     frames = lax.axis_size("frame")
     if fits_fused(mp_size, dp_size, frames, clips, spots, width, depth, heads_width):
         next_state, grad_proj = fused(
-            dp_size, tokens.reshape(clips, spots, width), token_mask, mask_embed.reshape(1, width), w_qkv.transpose(1, 0, 2), w_out,
+            dp_size, tokens.reshape(clips, spots, width), token_mask, mask_embed, w_qkv.transpose(1, 0, 2), w_out,
             cotangent.reshape(clips, spots, width), act_proj, codebook,
             action_idx.reshape(clips), frames)
         next_state, grad_proj = finish(next_state.reshape(2 * clips, spots // 2, width), grad_proj)

time: 217 us -> 214 us (0.986)
    pallas_call x1, Pallas kernels: 213 us -> 210 us  [fused(): pl.pallas_call(functools.partial(fused_kernel, dps), in_specs=[any_spec,...]
where the time goes in v6:
time: 214 us; the launch traced here: 213 us
  Pallas kernels  213 us (100%)
    pallas_call x1, Pallas kernels, fused(): pl.pallas_call(functools.partial(fused_kernel, dps), in_specs=[any_spec,...  210 us

profile of v6, /device:TPU:1, one launch (start us, length us, event | category | flops | bytes accessed | tf_op | source)
XLA Modules:
  0.0 213.4 jit_solution(9053404919061783876)
XLA Ops:
  0.6 210.4 %fused.1 = (bf16[2,160,2560]{2,1,0:T(8,128)(2,1)}, f32[32,2560]{1,0:T(8,128)}) custom-call(bf16[2,160,2560]{2,1,0:T(8,128)(2,1)} %bitcast.9, s32[2,1,160]{2,1,0:T(1,128)} %mask_ref.1, bf16[2560]{0:T(1024)(128)(2,1)} %embed_ref.1, bf16[3,640,1536]{2,1,0:T(8,128)(2,1)} %bitcast.8, bf16[1536,5120]{1,0:T(8,128)(2,1)} %o_ref.1, bf16[2,160,2560]{2,1,0:T(8,128)(2,1)} %bitcast.10, ...), custom_call_target="tpu_custom_call" | custom-call | tf_op jit(solution)/shard_map/fused/pallas_call | solution.py:702
  211.1 2.4 %finish.1 = (bf16[4,80,2560]{2,1,0:T(8,128)(2,1)}, f32[32,2560]{1,0:T(8,128)}) custom-call(bf16[4,80,2560]{2,1,0:T(8,128)(2,1)} %bitcast.11, f32[32,2560]{1,0:T(8,128)} %get-tuple-element.7.grad_ref), custom_call_target="tpu_custom_call" | custom-call | tf_op jit(solution)/shard_map/finish/pallas_call | solution.py:760

commit v7 on v6

--- a/solution.py
+++ b/solution.py
@@ -279,8 +279,26 @@
     own_x = pltpu.make_async_copy(xin.at[lo], xbuf.at[m, f], own_sem.at[per_group])
     for h in range(per_group):
         w_own(h).start()
-    for copy in loads:
-        copy.start()
+    loads[0].start()
+    pl.semaphore_wait(barrier, count)
+
+    last = per_group - 1
+    outer = jnp.logical_not(inner)
+
+    def send_tokens(q):
+        for k in range(1, lines):
+            x_direct(k, q).start()
+
+    def send_weights(h):
+        for k in range(4):
+            w_direct(h, k).start()
+
+    send_weights(0)
+
+    @pl.loop(0, slices)
+    def _(i):
+        o_across(i).start()
+
     loads[0].wait()
     gate[0:1, :] = embed_ref[...].astype(jnp.float32)[None, :]
     same = (lax.broadcasted_iota(jnp.int32, (spots, spots), 0)
@@ -296,28 +314,9 @@
                                         xin[r, :, cols].astype(jnp.float32)).astype(xin.dtype)
 
     own_x.start()
-    pl.semaphore_wait(barrier, count)
-
-    last = per_group - 1
-    outer = jnp.logical_not(inner)
-
-    def send_tokens(q):
-        for k in range(1, lines):
-            x_direct(k, q).start()
-
-    def send_weights(h):
-        for k in range(4):
-            w_direct(h, k).start()
-
-    send_weights(0)
     send_tokens(0)
 
-    @pl.loop(0, slices)
-    def _(i):
-        o_across(i).start()
-
-    for h in range(per_group):
-        w_partner(h).start()
+    w_partner(0).start()
 
     @pl.loop(0, pieces)
     def _(q):
@@ -326,6 +325,9 @@
     @pl.loop(0, 2)
     def _(j):
         forward_w(0, j)
+
+    for copy in loads[1:]:
+        copy.start()
 
     send_tokens(1)
 
@@ -413,6 +415,9 @@
     def ready_chip(h):
         w_own(h).wait()
         arrived(wbuf.at[h, :, whole_rows(other_core), :], w_recv.at[h, other_core, 0])
+
+    for h in range(1, per_group):
+        w_partner(h).start()
 
     @pl.loop(0, pieces + 3)
     def _(q):

time: 214 us -> 212 us (level)
  no operation moved by 1% of the time
where the time goes in v7:
time: 212 us
  Pallas kernels  211 us (100%)
    pallas_call x1, Pallas kernels, fused(): pl.pallas_call(functools.partial(fused_kernel, dps), in_specs=[any_spec,...  209 us

profile of v7, /device:TPU:1, one launch (start us, length us, event | category | flops | bytes accessed | tf_op | source)
XLA Modules:
  0.0 211.8 jit_solution(7244622649692927501)
XLA Ops:
  0.6 208.8 %fused.1 = (bf16[2,160,2560]{2,1,0:T(8,128)(2,1)}, f32[32,2560]{1,0:T(8,128)}) custom-call(bf16[2,160,2560]{2,1,0:T(8,128)(2,1)} %bitcast.9, s32[2,1,160]{2,1,0:T(1,128)} %mask_ref.1, bf16[2560]{0:T(1024)(128)(2,1)} %embed_ref.1, bf16[3,640,1536]{2,1,0:T(8,128)(2,1)} %bitcast.8, bf16[1536,5120]{1,0:T(8,128)(2,1)} %o_ref.1, bf16[2,160,2560]{2,1,0:T(8,128)(2,1)} %bitcast.10, ...), custom_call_target="tpu_custom_call" | custom-call | tf_op jit(solution)/shard_map/fused/pallas_call | solution.py:707
  209.5 2.4 %finish.1 = (bf16[4,80,2560]{2,1,0:T(8,128)(2,1)}, f32[32,2560]{1,0:T(8,128)}) custom-call(bf16[4,80,2560]{2,1,0:T(8,128)(2,1)} %bitcast.11, f32[32,2560]{1,0:T(8,128)} %get-tuple-element.7.grad_ref), custom_call_target="tpu_custom_call" | custom-call | tf_op jit(solution)/shard_map/finish/pallas_call | solution.py:765

commit v8 on v7

--- a/solution.py
+++ b/solution.py
@@ -241,17 +241,28 @@
     def a_own(h):
         return pltpu.make_async_copy(abuf.at[h, f], attn_block(m, f, h), a_recv.at[h, f])
 
-    def a_across(h, k):
-        owner = (f + frames - k) % frames
+    def a_across(h, owner):
         block = attn_block(m, owner, h)
         return remote(block, block, e_send, e_recv.at[h], mp=1 - m)
+
+    def forward_block(h, owner):
+        arrived(attn_block(m, owner, h), a_recv.at[h, owner])
+        a_across(h, owner).start()
 
     def forward_attn(h):
         @pl.loop(0, frames)
         def _(k):
-            owner = (f + frames - k) % frames
-            arrived(attn_block(m, owner, h), a_recv.at[h, owner])
-            a_across(h, k).start()
+            forward_block(h, (f + frames - k) % frames)
+
+    def forward_from_inner(h):
+        @pl.loop(frames // 4, frames - frames // 4)
+        def _(owner):
+            forward_block(h, owner)
+
+    def forward_from_outer(h):
+        @pl.loop(0, frames // 2)
+        def _(i):
+            forward_block(h, jnp.where(i < frames // 4, i, i + frames // 2))
 
     barrier = pltpu.get_barrier_semaphore()
     clips = xin.shape[0]
@@ -502,55 +513,6 @@
         o_core(q1, i, 3).start()
 
     attention(0, 0)
-
-    @pl.loop(0, last * frames)
-    def _(i):
-        h, jj = 1 + i // frames, i % frames
-
-        @pl.when(jnp.logical_and(inner, jnp.logical_and(h < last, jj >= 4)))
-        def _():
-            forward_w(h + 1, jj - 2)
-
-        @pl.when(jnp.logical_and(outer, jnp.logical_and(h < last, jj >= 6)))
-        def _():
-            forward_w(h + 1, jj - 4)
-
-        @pl.when(jnp.logical_and(outer, jnp.logical_and(h > 1, jnp.logical_and(jj >= 4, jj < 6))))
-        def _():
-            forward_w(h, jj)
-
-        @pl.when(jj == 0)
-        def _():
-            ready_chip(h)
-
-        @pl.when(jj >= 2)
-        def _():
-            with scope("w_y"):
-                ready_w(h, jnp.maximum(jj - 2, 0))
-
-        owner = jnp.where(jj == 0, f, jnp.where(jj == 1, other_core, source_of(jnp.maximum(jj - 2, 0))))
-        with scope("mm"):
-            matmul(0, h, owner, jj == 0)
-
-        @pl.when(jj == frames - 1)
-        def _():
-            attention(0, h)
-
-        @pl.when(jnp.logical_and(h == last, jj == 5))
-        def _():
-            with scope("fa"):
-                forward_attn(last - 1)
-
-        @pl.when(jnp.logical_and(h == last, jj == 3))
-        def _():
-            for before in range(last - 1):
-                with scope("fa"):
-                    forward_attn(before)
-
-    @pl.loop(0, slices)
-    def _(i):
-        for which in (d * 2 + 1 - c, (1 - d) * 2 + 1 - c):
-            arrived(o_piece(which, i), o_recv.at[which, i])
 
     for copy in loads[1:]:
         copy.wait()
@@ -569,6 +531,57 @@
     for half_of in range(2):
         mine_terms[half_of, :, side:] = marks
 
+    @pl.loop(0, last * frames)
+    def _(i):
+        h, jj = 1 + i // frames, i % frames
+
+        @pl.when(jnp.logical_and(inner, jnp.logical_and(h < last, jj >= 4)))
+        def _():
+            forward_w(h + 1, jj - 2)
+
+        @pl.when(jnp.logical_and(outer, jnp.logical_and(h < last, jj >= 6)))
+        def _():
+            forward_w(h + 1, jj - 4)
+
+        @pl.when(jnp.logical_and(outer, jnp.logical_and(h > 1, jnp.logical_and(jj >= 4, jj < 6))))
+        def _():
+            forward_w(h, jj)
+
+        @pl.when(jj == 0)
+        def _():
+            ready_chip(h)
+
+        @pl.when(jj >= 2)
+        def _():
+            with scope("w_y"):
+                ready_w(h, jnp.maximum(jj - 2, 0))
+
+        owner = jnp.where(jj == 0, f, jnp.where(jj == 1, other_core, source_of(jnp.maximum(jj - 2, 0))))
+        with scope("mm"):
+            matmul(0, h, owner, jj == 0)
+
+        @pl.when(jj == frames - 1)
+        def _():
+            attention(0, h)
+
+        @pl.when(jnp.logical_and(h == last, jj == 5))
+        def _():
+            with scope("fa"):
+                forward_attn(last - 1)
+
+        @pl.when(jnp.logical_and(h == last, jj == 3))
+        def _():
+            for before in range(last - 1):
+                with scope("fa"):
+                    forward_attn(before)
+
+    forward_from_inner(last)
+
+    @pl.loop(0, slices)
+    def _(i):
+        for which in (d * 2 + 1 - c, (1 - d) * 2 + 1 - c):
+            arrived(o_piece(which, i), o_recv.at[which, i])
+
     def partial(h, side, cols):
         w = jnp.concatenate(
             [wo[side, pl.ds(pl.multiple_of((g * per_group + h) * HS, HS), HS), cols]
@@ -580,11 +593,6 @@
 
     @pl.loop(0, last)
     def _(h):
-        @pl.when(h == last - 1)
-        def _():
-            with scope("fa"):
-                forward_attn(last)
-
         with scope("exchanged"):
             exchanged(h)
 
@@ -600,6 +608,8 @@
             @pl.when(h > 0)
             def _():
                 total[:, cols] += y
+
+    forward_from_outer(last)
 
     @pl.loop(0, width // tile)
     def _(n):

time: 212 us -> 211 us (level)
  no operation moved by 1% of the time
where the time goes in v8:
time: 211 us
  Pallas kernels  210 us (100%)
    pallas_call x1, Pallas kernels, fused(): pl.pallas_call(functools.partial(fused_kernel, dps), in_specs=[any_spec,...  208 us

profile of v8, /device:TPU:1, one launch (start us, length us, event | category | flops | bytes accessed | tf_op | source)
XLA Modules:
  0.0 210.9 jit_solution(2964297416828466850)
XLA Ops:
  0.6 207.9 %fused.1 = (bf16[2,160,2560]{2,1,0:T(8,128)(2,1)}, f32[32,2560]{1,0:T(8,128)}) custom-call(bf16[2,160,2560]{2,1,0:T(8,128)(2,1)} %bitcast.9, s32[2,1,160]{2,1,0:T(1,128)} %mask_ref.1, bf16[2560]{0:T(1024)(128)(2,1)} %embed_ref.1, bf16[3,640,1536]{2,1,0:T(8,128)(2,1)} %bitcast.8, bf16[1536,5120]{1,0:T(8,128)(2,1)} %o_ref.1, bf16[2,160,2560]{2,1,0:T(8,128)(2,1)} %bitcast.10, ...), custom_call_target="tpu_custom_call" | custom-call | tf_op jit(solution)/shard_map/fused/pallas_call | solution.py:717
  208.6 2.4 %finish.1 = (bf16[4,80,2560]{2,1,0:T(8,128)(2,1)}, f32[32,2560]{1,0:T(8,128)}) custom-call(bf16[4,80,2560]{2,1,0:T(8,128)(2,1)} %bitcast.11, f32[32,2560]{1,0:T(8,128)} %get-tuple-element.7.grad_ref), custom_call_target="tpu_custom_call" | custom-call | tf_op jit(solution)/shard_map/finish/pallas_call | solution.py:775

commit v9 on v8

--- a/solution.py
+++ b/solution.py
@@ -569,7 +569,7 @@
             with scope("fa"):
                 forward_attn(last - 1)
 
-        @pl.when(jnp.logical_and(h == last, jj == 3))
+        @pl.when(jnp.logical_and(h == last, jj == 1))
         def _():
             for before in range(last - 1):
                 with scope("fa"):

time: 211 us -> 211 us (level)
  no operation moved by 1% of the time
where the time goes in v9:
time: 211 us
  Pallas kernels  210 us (100%)
    pallas_call x1, Pallas kernels, fused(): pl.pallas_call(functools.partial(fused_kernel, dps), in_specs=[any_spec,...  208 us

profile of v9, /device:TPU:1, one launch (start us, length us, event | category | flops | bytes accessed | tf_op | source)
XLA Modules:
  0.0 210.9 jit_solution(9007260254679106004)
XLA Ops:
  0.6 207.9 %fused.1 = (bf16[2,160,2560]{2,1,0:T(8,128)(2,1)}, f32[32,2560]{1,0:T(8,128)}) custom-call(bf16[2,160,2560]{2,1,0:T(8,128)(2,1)} %bitcast.9, s32[2,1,160]{2,1,0:T(1,128)} %mask_ref.1, bf16[2560]{0:T(1024)(128)(2,1)} %embed_ref.1, bf16[3,640,1536]{2,1,0:T(8,128)(2,1)} %bitcast.8, bf16[1536,5120]{1,0:T(8,128)(2,1)} %o_ref.1, bf16[2,160,2560]{2,1,0:T(8,128)(2,1)} %bitcast.10, ...), custom_call_target="tpu_custom_call" | custom-call | tf_op jit(solution)/shard_map/fused/pallas_call | solution.py:717
  208.6 2.4 %finish.1 = (bf16[4,80,2560]{2,1,0:T(8,128)(2,1)}, f32[32,2560]{1,0:T(8,128)}) custom-call(bf16[4,80,2560]{2,1,0:T(8,128)(2,1)} %bitcast.11, f32[32,2560]{1,0:T(8,128)} %get-tuple-element.7.grad_ref), custom_call_target="tpu_custom_call" | custom-call | tf_op jit(solution)/shard_map/finish/pallas_call | solution.py:775
